TPU v7x, 256 devices: a whole 4x4x8 slice. The times are simulated.
256 devices in a mesh: grp: 8 (over x, core), dp: 32 (over y, z).
Axes of the slice: x: 4, y: 4, z: 8, core: 2. Of those that a mesh axis runs over, the one named last changes fastest.
Arguments:
- chosen_ids: int32 [256, 512], P(('grp', 'dp')), may hold values from 0 to 128255, as said below
- rejected_ids: int32 [256, 512], P(('grp', 'dp')), may hold values from 0 to 128255, as said below
- chosen_len: int32 [256], P(('grp', 'dp')), may hold values from 64 to 256
- rejected_len: int32 [256], P(('grp', 'dp')), may hold values from 64 to 256
- chosen_logp: float32 [256, 512], P(('grp', 'dp')), may hold values from -0.3 to -0.01
- rejected_logp: float32 [256, 512], P(('grp', 'dp')), may hold values from -0.3 to -0.01
- ref_logp: float32 [2, 256], P(None, ('grp', 'dp')), may hold values from -40 to -10
- chosen_grads: bfloat16 [256, 512, 4096], P(('grp', 'dp')), may hold values from -48 to 48
- rejected_grads: bfloat16 [256, 512, 4096], P(('grp', 'dp')), may hold values from -48 to 48
Outputs:
- grad_table: bfloat16 [128256, 4096], P(('grp', 'dp'))
Inputs may be any that keep to these rules, and one draw needn't show every extreme that they name: `chosen_ids`: vocabulary row v belongs to owner v // 501. The chosen and rejected tokens of one device's pairs together fall at most 6 times into one owner's rows; 16 owners drawn from the seed get exactly 6 of them from every device. `rejected_ids`: drawn together with chosen_ids under the same bound. The response is the last chosen_len[p] positions of the sequence. The response is the last rejected_len[p] positions of the sequence.
All inputs are finite; a program needn't handle non-finite values.
Results may differ from a plain program's by a relative error of at most 0.001.
The roundings to bfloat16 on the way count: a program that leaves them out, or rounds other values in their place, can miss the bound.
Values may be sent and summed in bfloat16 or wider, within the bound.
No kernel may reach another device: no remote copies, remote signals or barrier semaphores. Data moves between devices by JAX's collectives and lax.ppermute only.
A program may use at most 128 MiB of HBM per device.

v0:
```python
import functools

import jax
import jax.numpy as jnp
from jax import lax
from jax.experimental import pallas as pl
from jax.experimental.pallas import tpu as pltpu
from jax.sharding import PartitionSpec as P


VOCAB = 128256
BETA = 0.1
XS, CORES, YS, ZS = 4, 2, 4, 8
PLANE = XS * CORES * YS
CAP = 6
DIRECT = 4
REST = CAP - DIRECT
LIMIT = 32
UNITS = 4
NOTE = 128
FLAG, ROUTE = 12, 13
STEP = 512
WIDE = 1024
CHUNK = 512
TURNS = XS * YS

bf16 = jnp.bfloat16
f32 = jnp.float32
i32 = jnp.int32


def iota(shape, dim):
    return lax.broadcasted_iota(i32, shape, dim)


def onehot(hit):
    return jnp.where(hit, 1.0, 0.0).astype(bf16)


def dot(a, b):
    return jnp.dot(a, b, preferred_element_type=f32)


def dot_t(a, b):
    return lax.dot_general(a, b, (((1,), (1,)), ((), ())), preferred_element_type=f32)


def before(hits):
    tokens = hits.shape[1]
    block = 256
    earlier = onehot(iota((block, block), 0) < iota((block, block), 1))
    carry = jnp.zeros((hits.shape[0], 1), f32)
    counts = []
    for b in range(0, tokens, block):
        piece = hits[:, b : b + block]
        counts.append(dot(piece.astype(bf16), earlier) + carry)
        carry = carry + jnp.sum(piece, axis=1, keepdims=True)
    return jnp.concatenate(counts, axis=1)


def here():
    grp = lax.axis_index("grp")
    dp = lax.axis_index("dp")
    return dp & (ZS - 1), grp // CORES, grp & (CORES - 1), dp // ZS


def route(cid, rid, plan, note, row_count):
    ids = jnp.concatenate([cid[...], rid[...]], axis=1)
    owner = jnp.floor((ids.astype(f32) + 0.5) * (1.0 / row_count)).astype(i32)
    row = ids - owner * row_count
    mate = owner // ZS
    shift = (owner - here()[0]) & (ZS - 1)
    tokens = ids.shape[1]
    owners = PLANE * ZS
    near = jnp.where(iota((owners, tokens), 0) == shift * PLANE + mate, 1.0, 0.0)
    rank = jnp.sum(near * before(near), axis=0, keepdims=True).astype(i32)
    rest = rank >= DIRECT
    by_shift = jnp.where((iota((ZS, tokens), 0) == shift) & rest, 1.0, 0.0)
    order = jnp.sum(by_shift * before(by_shift), axis=0, keepdims=True).astype(i32)
    late = rest & (order >= LIMIT)
    first = jnp.where(rest & (order < LIMIT), shift * LIMIT + order, -1)
    plan[0:1] = jnp.where(rest, -1, owner * DIRECT + rank)
    plan[1:2] = first
    plan[2:3] = jnp.where(late, owner * REST + rank - DIRECT, -1)
    plan[3:8] = jnp.zeros((5, tokens), i32)
    over = jnp.max(jnp.where(late, 1.0, 0.0), axis=1, keepdims=True)
    lane = iota((NOTE, tokens), 0)
    code = jnp.where(lane == 2 * rank, row >> 4, 0) + jnp.where(lane == 2 * rank + 1, row & 15, 0)
    labels = dot_t(near.astype(bf16), code.astype(f32).astype(bf16))
    way = jnp.where(lane == ROUTE, mate * REST + (rank - DIRECT) + 1, 0)
    moved = onehot(iota((ZS * LIMIT, tokens), 0) == first)
    ways = dot_t(moved, way.astype(f32).astype(bf16))
    flag = jnp.where(iota((owners, NOTE), 1) == FLAG, over, 0.0)
    note[...] = (labels + ways + flag).astype(bf16)


def pair_weight(clen, rlen, clogp, rlogp, ref):
    length = clogp.shape[1]
    positions = iota((1, length), 1)
    chosen_mask = (positions >= length - clen[0]).astype(f32)
    rejected_mask = (positions >= length - rlen[0]).astype(f32)
    chosen = jnp.sum(chosen_mask * clogp[...], axis=1, keepdims=True)
    rejected = jnp.sum(rejected_mask * rlogp[...], axis=1, keepdims=True)
    margin = BETA * ((chosen - ref[0]) - (rejected - ref[1]))
    return BETA * (1.0 / (1.0 + jnp.exp(margin)))


def weighted(weight, cg, rg, rows):
    half = cg.shape[1]
    rows[:half] = (-weight[0:1, 0:1] * cg[0].astype(f32)).astype(bf16)
    rows[half:] = (weight[0:1, 0:1] * rg[0].astype(f32)).astype(bf16)


def first_kernel(cid, rid, clen, rlen, clogp, rlogp, ref, cg, rg, *refs, row_count):
    outs = refs[:ZS]
    plan, weight, note, pick = refs[ZS:]
    step = pl.program_id(0)
    last = pl.num_programs(0) - 1

    @pl.when(step == 0)
    def _():
        route(cid, rid, plan, note, row_count)
        weight[...] = jnp.broadcast_to(
            pair_weight(clen, rlen, clogp, rlogp, ref), weight.shape
        )
        pick[...] = onehot(iota(pick.shape, 0) == plan[1:2])

    @pl.when(step < last)
    def _():
        half = cg.shape[1]
        scale = weight[0:1, 0:1]
        moved = dot(pick[:, :half], cg[0]) * -scale + dot(pick[:, half:], rg[0]) * scale
        moved = moved.astype(bf16)
        for d in range(ZS):
            outs[d][...] = moved[d * LIMIT : d * LIMIT + LIMIT]

    @pl.when(step == last)
    def _():
        for d in range(ZS):
            outs[d][:, :NOTE] = note[d * LIMIT : d * LIMIT + LIMIT]


def direct_kernel(plan, weight, cg, rg, out, rows, pick, wide, *, kind):
    step = pl.program_id(0)

    @pl.when(step == 0)
    def _():
        pick[...] = onehot(iota(pick.shape, 0) == plan[kind : kind + 1])

    weighted(weight, cg, rg, rows)
    width = out.shape[1]
    slots = pick.shape[0]
    moved = dot(pick[...], rows[...])
    for u in range(UNITS):
        wide[pl.ds(u, slots, stride=UNITS), :] = moved[:, u * width : (u + 1) * width]
    out[...] = wide[...].astype(bf16)


def turned(turn, swap, place):
    y = (turn + place[3]) & (YS - 1)
    core = (swap + place[2]) & (CORES - 1)
    x = (turn // YS + place[1]) & (XS - 1)
    return (x * CORES + core) * YS + y


def second_kernel(*refs):
    place = here()
    arrived = refs[:ZS]
    notes = refs[ZS : 2 * ZS]
    outs = refs[2 * ZS : 2 * ZS + TURNS]
    pick, spread = refs[2 * ZS + TURNS :]
    step = pl.program_id(0)
    last = pl.num_programs(0) - 1
    each = ZS * REST
    both = CORES * each

    @pl.when(step == 0)
    def _():
        note = jnp.concatenate([n[...] for n in notes], axis=0).astype(f32)
        blocks = [jnp.transpose(note[b : b + 128]) for b in range(0, ZS * LIMIT, 128)]
        way = jnp.concatenate(blocks, axis=1)[ROUTE : ROUTE + 1].astype(i32)
        out_row = iota(pick.shape, 0)
        in_row = iota(pick.shape, 1)
        mate = turned(out_row // both, out_row // each, place)
        shift = (out_row // REST) & (ZS - 1)
        wanted = mate * REST + (out_row & (REST - 1)) + 1
        pick[...] = onehot((in_row // LIMIT == shift) & (way == wanted))
        spread[...] = onehot(in_row == shift * PLANE + mate)

    @pl.when(step < last)
    def _():
        rows = jnp.concatenate([a[...] for a in arrived], axis=0)
        moved = dot(pick[...], rows).astype(bf16)
        for e in range(TURNS):
            outs[e][...] = moved[e * both : e * both + both]

    @pl.when(step == last)
    def _():
        note = jnp.concatenate([n[...] for n in notes], axis=0)
        moved = dot(spread[...], note).astype(bf16)
        for e in range(TURNS):
            outs[e][:, :NOTE] = moved[e * both : e * both + both]


def stack_kernel(*refs):
    out = refs[-1]
    for i, part in enumerate(refs[:-1]):
        out[i * part.shape[0] : (i + 1) * part.shape[0]] = part[...]


def collect_kernel(*refs):
    place = here()
    parts = refs[: TURNS + 1]
    notes = refs[TURNS + 1 : 2 * TURNS + 2]
    rows, near, far, late, flag = refs[2 * TURNS + 2 :]
    each = ZS * REST
    count = PLANE * each
    owners = PLANE * ZS
    start = 0
    for part in parts:
        rows[start : start + part.shape[0]] = part[...]
        start += part.shape[0]

    @pl.when(pl.program_id(0) == 0)
    def _():
        note = jnp.concatenate([n[...] for n in notes], axis=0)
        wide = note.astype(f32)
        across = jnp.concatenate(
            [jnp.transpose(wide[b : b + 128]) for b in range(0, count, 128)], axis=1
        )
        flag[0] = jnp.max(across[FLAG : FLAG + 1]).astype(i32)

        def joined(across, ranks):
            which = iota((1, across.shape[1]), 1) % len(ranks)
            found = jnp.zeros(which.shape, f32)
            for i, rank in enumerate(ranks):
                high = across[2 * rank : 2 * rank + 1]
                low = across[2 * rank + 1 : 2 * rank + 2]
                found = found + jnp.where(which == i, 16.0 * high + low, 0.0)
            return found.astype(i32)

        straight = range(DIRECT)
        others = range(DIRECT, CAP)
        far[...] = joined(across, others)
        source = iota((owners, count), 0)
        item = iota((owners, count), 1)
        turn = item // each
        y = (place[3] - turn) & (YS - 1)
        x = (place[1] - turn // YS) & (XS - 1)
        core = (place[2] - turn // TURNS) & (CORES - 1)
        z = (place[0] - item // REST) & (ZS - 1)
        match = (source == ((x * CORES + core) * YS + y) * ZS + z) & ((item & (REST - 1)) == 0)
        by_source = dot(onehot(match), note).astype(bf16)
        for out, ranks in ((near, straight), (late, others)):
            places = owners * len(ranks)
            grow = onehot(iota((owners, places), 1) // len(ranks) == iota((owners, places), 0))
            grown = lax.dot_general(
                by_source, grow, (((0,), (0,)), ((), ())), preferred_element_type=f32
            )
            out[...] = joined(grown, ranks)


def finish_kernel(*refs, tiled):
    labels = refs[: tiled + 1]
    packed = refs[tiled + 1 : 2 * tiled + 1]
    rest = refs[2 * tiled + 1]
    out, pick, *scratch = refs[2 * tiled + 2 :]
    step = pl.program_id(0)
    half = CHUNK

    @pl.when(step == 0)
    def _():
        start = 0
        for label in labels:
            size = label.shape[1]
            block = pick.at[:, start : start + size]
            block[...] = onehot(iota(block.shape, 0) == label[...])
            start += size

    total = dot(pick[:, -rest.shape[0] :], rest[...])
    start = 0
    for block in packed:
        width = block.shape[1]
        for first in range(0, block.shape[0] // UNITS, half):
            wide, rows = scratch[2 * (start // half % 2) : 2 * (start // half % 2) + 2]
            wide[...] = block[first * UNITS : (first + half) * UNITS].astype(f32)
            for u in range(UNITS):
                rows[:, u * width : (u + 1) * width] = wide[
                    pl.ds(u, half, stride=UNITS), :
                ].astype(bf16)
            total += dot(pick[:, start : start + half], rows[...])
            start += half
    out[...] = total[: out.shape[0]].astype(bf16)


def shifted(dx, dcore, dy, dz):
    def at(x, core, y, z):
        return ((x % XS * CORES + core % CORES) * YS + y % YS) * ZS + z % ZS

    return [
        (at(x, core, y, z), at(x + dx, core + dcore, y + dy, z + dz))
        for x in range(XS)
        for core in range(CORES)
        for y in range(YS)
        for z in range(ZS)
    ]


def whole(*shape):
    return pl.BlockSpec(shape, lambda *_: (0,) * len(shape))


def local(cid, rid, clen, rlen, clogp, rlogp, ref, cg, rg):
    length, features = cg.shape[1:]
    tokens = 2 * length
    owners = PLANE * ZS
    row_count = VOCAB // owners
    axes = ("grp", "dp")
    smem = pl.BlockSpec(memory_space=pltpu.SMEM)
    columns = features + NOTE
    steps = features // STEP
    width = STEP // UNITS
    each = ZS * REST
    padded = (row_count + 15) // 16 * 16

    few = features // WIDE
    part = pl.BlockSpec((1, length, WIDE), lambda n: (0, 0, jnp.minimum(n, few - 1)))
    *first, plan, weight = pl.pallas_call(
        functools.partial(first_kernel, row_count=row_count),
        out_shape=[jax.ShapeDtypeStruct((LIMIT, columns), bf16)] * ZS
        + [jax.ShapeDtypeStruct((8, tokens), i32), jax.ShapeDtypeStruct((8, 128), f32)],
        grid=(few + 1,),
        in_specs=[whole(1, length)] * 2
        + [smem] * 2
        + [whole(1, length)] * 2
        + [smem, part, part],
        out_specs=[pl.BlockSpec((LIMIT, WIDE), lambda n: (0, n))] * ZS
        + [whole(8, tokens), whole(8, 128)],
        scratch_shapes=[
            pltpu.VMEM((owners, NOTE), bf16),
            pltpu.VMEM((ZS * LIMIT, tokens), bf16),
        ],
        name="first",
    )(cid, rid, clen, rlen, clogp, rlogp, ref.reshape(2), cg, rg)
    hopped = [first[0]] + [
        lax.ppermute(first[d], axes, shifted(0, 0, 0, d)) for d in range(1, ZS)
    ]

    def direct(kind, count):
        slots = owners * count
        sent = pl.pallas_call(
            functools.partial(direct_kernel, kind=kind),
            out_shape=jax.ShapeDtypeStruct((slots * UNITS, features // UNITS), bf16),
            grid=(steps,),
            in_specs=[
                whole(8, tokens),
                whole(8, 128),
                pl.BlockSpec((1, length, STEP), lambda n: (0, 0, n)),
                pl.BlockSpec((1, length, STEP), lambda n: (0, 0, n)),
            ],
            out_specs=pl.BlockSpec((slots * UNITS, width), lambda n: (0, n)),
            scratch_shapes=[
                pltpu.VMEM((tokens, STEP), bf16),
                pltpu.VMEM((slots, tokens), bf16),
                pltpu.VMEM((slots * UNITS, width), f32),
            ],
            name="direct",
        )(plan, weight, cg, rg)
        sent = sent.reshape(owners, count * UNITS, features // UNITS)
        sent = lax.all_to_all(sent, axes, split_axis=0, concat_axis=0, tiled=True)
        return sent.reshape(slots * UNITS, features // UNITS)

    arrived = direct(0, DIRECT)

    both = CORES * each
    here_part = [pl.BlockSpec((LIMIT, WIDE), lambda n: (0, jnp.minimum(n, few - 1)))] * ZS
    here_note = [pl.BlockSpec((LIMIT, NOTE), lambda n: (0, features // NOTE))] * ZS
    second = pl.pallas_call(
        second_kernel,
        out_shape=[jax.ShapeDtypeStruct((both, columns), bf16)] * TURNS,
        grid=(few + 1,),
        in_specs=here_part + here_note,
        out_specs=[pl.BlockSpec((both, WIDE), lambda n: (0, n))] * TURNS,
        scratch_shapes=[
            pltpu.VMEM((PLANE * each, ZS * LIMIT), bf16),
            pltpu.VMEM((PLANE * each, ZS * LIMIT), bf16),
        ],
        name="second",
    )(*hopped, *hopped)
    turns = [second[0]] + [
        lax.ppermute(second[e], axes, shifted(e // YS, 0, e % YS, 0)) for e in range(1, TURNS)
    ]
    swap = pl.pallas_call(
        stack_kernel,
        out_shape=jax.ShapeDtypeStruct((TURNS * each, columns), bf16),
        grid=(few + 1,),
        in_specs=[pl.BlockSpec((each, WIDE), lambda n: (1, n))] * TURNS,
        out_specs=pl.BlockSpec((TURNS * each, WIDE), lambda n: (0, n)),
        name="stack",
    )(*turns)
    swap = lax.ppermute(swap, axes, shifted(0, 1, 0, 0))

    rest, near, far, late, flag = pl.pallas_call(
        collect_kernel,
        out_shape=[
            jax.ShapeDtypeStruct((PLANE * each, features), bf16),
            jax.ShapeDtypeStruct((1, owners * DIRECT), i32),
            jax.ShapeDtypeStruct((1, PLANE * each), i32),
            jax.ShapeDtypeStruct((1, owners * REST), i32),
            jax.ShapeDtypeStruct((1,), i32),
        ],
        grid=(few,),
        in_specs=[pl.BlockSpec((each, WIDE), lambda n: (0, n))] * TURNS
        + [pl.BlockSpec((TURNS * each, WIDE), lambda n: (0, n))]
        + [pl.BlockSpec((each, NOTE), lambda n: (0, features // NOTE))] * TURNS
        + [pl.BlockSpec((TURNS * each, NOTE), lambda n: (0, features // NOTE))],
        out_specs=[
            pl.BlockSpec((PLANE * each, WIDE), lambda n: (0, n)),
            whole(1, owners * DIRECT),
            whole(1, PLANE * each),
            whole(1, owners * REST),
            smem,
        ],
        name="collect",
    )(*turns, swap, *turns, swap)

    def finish(labels, packed):
        count = sum(label.shape[1] for label in labels)
        return pl.pallas_call(
            functools.partial(finish_kernel, tiled=len(packed)),
            out_shape=jax.ShapeDtypeStruct((row_count, features), bf16),
            grid=(steps,),
            in_specs=[whole(*label.shape) for label in labels]
            + [pl.BlockSpec((block.shape[0], width), lambda n: (0, n)) for block in packed]
            + [pl.BlockSpec((PLANE * each, STEP), lambda n: (0, n))],
            out_specs=pl.BlockSpec((row_count, STEP), lambda n: (0, n)),
            scratch_shapes=[pltpu.VMEM((padded, count), bf16)]
            + [
                pltpu.VMEM((CHUNK * UNITS, width), f32),
                pltpu.VMEM((CHUNK, STEP), bf16),
            ]
            * 2,
            name="finish",
        )(*labels, *packed, rest)

    return lax.cond(
        flag[0] > 0,
        lambda: finish([near, late, far], [arrived, direct(2, REST)]),
        lambda: finish([near, far], [arrived]),
    )


def solution(mesh):
    return jax.shard_map(
        local,
        mesh=mesh,
        in_specs=(
            P(("grp", "dp"), None),
            P(("grp", "dp"), None),
            P(("grp", "dp")),
            P(("grp", "dp")),
            P(("grp", "dp"), None),
            P(("grp", "dp"), None),
            P(None, ("grp", "dp")),
            P(("grp", "dp"), None, None),
            P(("grp", "dp"), None, None),
        ),
        out_specs=P(("grp", "dp"), None),
        check_vma=False,
    )
```

profile of v0, /device:TPU:1, one launch (start us, length us, event | category | flops | bytes accessed | tf_op | source)
XLA Modules:
  0.0 392.4 jit_solution(12582254691593682329)
XLA Ops:
  1.3 7.9 %first.1 = (bf16[32,4224]{1,0:T(8,128)(2,1)}, bf16[32,4224]{1,0:T(8,128)(2,1)}, bf16[32,4224]{1,0:T(8,128)(2,1)}, bf16[32,4224]{1,0:T(8,128)(2,1)}, bf16[32,4224...) custom-call(s32[1,512]{1,0:T(1,128)} %cid.1, ...), custom_call_target="tpu_custom_call" | custom-call | tf_op jit(solution)/shard_map/first/pallas_call | solution.py:328
  9.2 14.6 %direct.3 = bf16[4096,1024]{1,0:T(8,128)(2,1)} custom-call(s32[8,1024]{1,0:T(8,128)S(1)} %get-tuple-element.105.plan, f32[8,128]{1,0:T(8,128)S(1)} %get-tuple-element.106.weight, bf16[1,512,4096]{2,1,0:T(8,128)(2,1)} %cg.3, bf16[1,512,4096]{2,1,0:T(8,128)(2,1)} %rg.3), custom_call_target="tpu_custom_call" | custom-call | tf_op jit(solution)/shard_map/direct/pallas_call | solution.py:351
  23.8 16.7 %all-to-all-start.1 = ((bf16[256,16,1024]{2,1,0:T(8,128)(2,1)}), bf16[256,16,1024]{2,1,0:T(8,128)(2,1)}, u32[]{:S(2)}, u32[]{:S(2)}) async-start(bf16[256,16,1024]{2,1,0:T(8,128)(2,1)} %bitcast.6), calls=%async_computation.1 | async-start | bytes 16777216 | tf_op jit(solution)/shard_map/all_to_all | solution.py:370
  42.0 2.6 collective-permute-start.1
  44.6 3.2 collective-permute-start.2
  48.8 3.7 collective-permute-start.4
  52.6 175.7 %collective-permute-done.refs_1_.refs_9_ = bf16[32,4224]{1,0:T(8,128)(2,1)S(1)} collective-permute-done((bf16[32,4224]{1,0:T(8,128)(2,1)S(1)}, bf16[32,4224]{1,0:T(8,128)(2,1)S(1)}, u32[]{:S(2)}, u32[]{:S(2)}) %collective-permute-start) | collective-permute-done | bytes 270368 | tf_op jit(solution)/shard_map/ppermute | solution.py:346
  230.1 8.4 %collective-permute-done.1.refs_2_.refs_10_ = bf16[32,4224]{1,0:T(8,128)(2,1)S(1)} collective-permute-done((bf16[32,4224]{1,0:T(8,128)(2,1)S(1)}, bf16[32,4224]{1,0:T(8,128)(2,1)S(1)}, u32[]{:S(2)}, u32[]{:S(2)}) %collective-permute-start.1) | collective-permute-done | bytes 270368 | tf_op jit(solution)/shard_map/ppermute | solution.py:346
  240.8 18.6 %collective-permute-done.2.refs_3_.refs_11_ = bf16[32,4224]{1,0:T(8,128)(2,1)S(1)} collective-permute-done((bf16[32,4224]{1,0:T(8,128)(2,1)S(1)}, bf16[32,4224]{1,0:T(8,128)(2,1)S(1)}, u32[]{:S(2)}, u32[]{:S(2)}) %collective-permute-start.2) | collective-permute-done | bytes 270368 | tf_op jit(solution)/shard_map/ppermute | solution.py:346
  259.4 11.2 %collective-permute-done.3.refs_4_.refs_12_ = bf16[32,4224]{1,0:T(8,128)(2,1)S(1)} collective-permute-done((bf16[32,4224]{1,0:T(8,128)(2,1)S(1)}, bf16[32,4224]{1,0:T(8,128)(2,1)S(1)}, u32[]{:S(2)}, u32[]{:S(2)}) %collective-permute-start.3) | collective-permute-done | bytes 270368 | tf_op jit(solution)/shard_map/ppermute | solution.py:346
  271.6 6.0 %second.1 = (bf16[32,4224]{1,0:T(8,128)(2,1)}, bf16[32,4224]{1,0:T(8,128)(2,1)}, bf16[32,4224]{1,0:T(8,128)(2,1)}, bf16[32,4224]{1,0:T(8,128)(2,1)}, bf16[32,422...) custom-call(bf16[32,4224]{1,0:T(8,128)(2,1)} %get-tuple-element.78.r, ...), custom_call_target="tpu_custom_call" | custom-call | tf_op jit(solution)/shard_map/second/pallas_call | solution.py:378
  280.4 16.7 %collective-permute-done.7.refs_1_.refs_18_ = bf16[32,4224]{1,0:T(8,128)(2,1)S(1)} collective-permute-done((bf16[32,4224]{1,0:T(8,128)(2,1)}, bf16[32,4224]{1,0:T(8,128)(2,1)S(1)}, u32[]{:S(2)}, u32[]{:S(2)}) %collective-permute-start.7) | collective-permute-done | bytes 270368 | tf_op jit(solution)/shard_map/ppermute | solution.py:391
  297.4 9.8 %collective-permute-start.16 = (bf16[32,4224]{1,0:T(8,128)(2,1)}, bf16[32,4224]{1,0:T(8,128)(2,1)S(1)}, u32[]{:S(2)}, u32[]{:S(2)}) collective-permute-start(bf16[32,4224]{1,0:T(8,128)(2,1)} %get-tuple-element.96), channel_id=1, source_target_pairs={{0,144},{1,145},{2,146},{3,147},{4,148},{5,149},{6,150},{7,151},{8... | collective-permute-start | bytes 811016 | tf_op jit(solution)/shard_map/ppermute | solution.py:391
  307.3 25.5 %collective-permute-done.13.refs_7_.refs_24_ = bf16[32,4224]{1,0:T(8,128)(2,1)S(1)} collective-permute-done((bf16[32,4224]{1,0:T(8,128)(2,1)}, bf16[32,4224]{1,0:T(8,128)(2,1)S(1)}, u32[]{:S(2)}, u32[]{:S(2)}) %collective-permute-start.13) | collective-permute-done | bytes 270368 | tf_op jit(solution)/shard_map/ppermute | solution.py:391
  332.9 3.6 collective-permute-start.20
  338.3 6.2 %collective-permute-done.19.refs_13_.refs_30_ = bf16[32,4224]{1,0:T(8,128)(2,1)S(1)} collective-permute-done((bf16[32,4224]{1,0:T(8,128)(2,1)}, bf16[32,4224]{1,0:T(8,128)(2,1)S(1)}, u32[]{:S(2)}, u32[]{:S(2)}) %collective-permute-start.19) | collective-permute-done | bytes 270368 | tf_op jit(solution)/shard_map/ppermute | solution.py:391
  344.5 3.8 collective-permute-done.20.refs_14_.refs_31_
  348.2 11.0 %collective-permute-done.21.refs_15_.refs_32_ = bf16[32,4224]{1,0:T(8,128)(2,1)} collective-permute-done((bf16[32,4224]{1,0:T(8,128)(2,1)}, bf16[32,4224]{1,0:T(8,128)(2,1)}, u32[]{:S(2)}, u32[]{:S(2)}) %collective-permute-start.21) | collective-permute-done | bytes 270368 | tf_op jit(solution)/shard_map/ppermute | solution.py:391
  359.3 4.1 %stack.1 = bf16[256,4224]{1,0:T(8,128)(2,1)} custom-call(bf16[32,4224]{1,0:T(8,128)(2,1)} %get-tuple-element.86.refs_0_.refs_17_, bf16[32,4224]{1,0:T(8,128)(2,1)} %copy-done.1, bf16[32,4224]{1,0:T(8,128)(2,1)} %copy-done.2, bf16[32,4224]{1,0:T(8,128)(2,1)} %copy-done.3, bf16[32,4224]{1,0:T(8,128)(2,1)} %copy-done.4, bf16[32,4224]{1,0:T(8,128)(2,1)} %copy-done.5, ...), custom_call_target="tpu_custom_call" | custom-call | tf_op jit(solution)/shard_map/stack/pallas_call | solution.py:393
  363.4 3.9 collective-permute-start.22
  367.3 4.1 %collective-permute-done.22.refs_16_.refs_33_ = bf16[256,4224]{1,0:T(8,128)(2,1)S(1)} collective-permute-done((bf16[256,4224]{1,0:T(8,128)(2,1)}, bf16[256,4224]{1,0:T(8,128)(2,1)S(1)}, u32[]{:S(2)}, u32[]{:S(2)}) %collective-permute-start.22) | collective-permute-done | bytes 2162720 | tf_op jit(solution)/shard_map/ppermute | solution.py:401
  372.8 5.6 %collect.1 = (bf16[512,4096]{1,0:T(8,128)(2,1)}, s32[1,1024]{1,0:T(1,128)S(1)}, s32[1,512]{1,0:T(1,128)S(1)}, s32[1,512]{1,0:T(1,128)S(1)}, s32[1]{0:T(128)}) custom-call(bf16[32,4224]{1,0:T(8,128)(2,1)} %get-tuple-element.86.refs_0_.refs_17_, bf16[32,4224]{1,0:T(8,128)(2,1)} %copy-done.1, bf16[32,4224]{1,0:T(8,128)(2,1)} %copy-done.2, ...), custom_call_target="tpu_custom_call" | custom-call | tf_op jit(solution)/shard_map/collect/pallas_call | solution.py:403
  379.0 13.4 %conditional.1 = (bf16[501,4096]{1,0:T(8,128)(2,1)}) conditional(s32[]{:T(128)} %bitcast.3, (s32[1,1024]{1,0:T(1,128)S(1)}, s32[1,512]{1,0:T(1,128)S(1)}, bf16[4096,1024]{1,0:T(8,128)(2,1)}, bf16[512,4096]{1,0:T(8,128)(2,1)}) %tuple.11, (s32[8,1024]{1,0:T(8,128)S(1)}, f32[8,128]{1,0:T(8,128)S(1)}, bf16[1,512,4096]{2,1,0:T(8,128)(2,1)}, ...), branch_computations={%region_0.0_spmd, %region_1.0_spmd} | conditional | bytes 8388616 | solution.py:446
  379.2 13.2 %finish.2 = bf16[501,4096]{1,0:T(8,128)(2,1)} custom-call(s32[1,1024]{1,0:T(1,128)S(1)} %get-tuple-element.34.refs_0_, s32[1,512]{1,0:T(1,128)S(1)} %get-tuple-element.35.refs_1_, bf16[4096,1024]{1,0:T(8,128)(2,1)} %get-tuple-element.36.refs_2_, bf16[512,4096]{1,0:T(8,128)(2,1)} %get-tuple-element.37.refs_3_), custom_call_target="tpu_custom_call" | custom-call | tf_op jit(solution)/shard_map/cond/branch_0_fun/finish/pallas_call | solution.py:429
  (87 shorter events, 13.9 us)
Async XLA Ops:
  23.8 355.2 %all-to-all-start.1 = ((bf16[256,16,1024]{2,1,0:T(8,128)(2,1)}), bf16[256,16,1024]{2,1,0:T(8,128)(2,1)}, u32[]{:S(2)}, u32[]{:S(2)}) async-start(bf16[256,16,1024]{2,1,0:T(8,128)(2,1)} %bitcast.6), calls=%async_computation.1 | async-start | bytes 16777216 | tf_op jit(solution)/shard_map/all_to_all | solution.py:370
  40.5 187.9 %collective-permute-start = (bf16[32,4224]{1,0:T(8,128)(2,1)S(1)}, bf16[32,4224]{1,0:T(8,128)(2,1)S(1)}, u32[]{:S(2)}, u32[]{:S(2)}) collective-permute-start(bf16[32,4224]{1,0:T(8,128)(2,1)S(1)} %copy-done.27), channel_id=1, source_target_pairs={{0,1},{1,2},{2,3},{3,4},{4,5},{5,6},{6,7},{7,0},{8,9},{9,10},{10,1... | collective-permute-start | bytes 811016 | tf_op jit(solution)/shard_map/ppermute | solution.py:346
  42.0 196.5 %collective-permute-start.1 = (bf16[32,4224]{1,0:T(8,128)(2,1)S(1)}, bf16[32,4224]{1,0:T(8,128)(2,1)S(1)}, u32[]{:S(2)}, u32[]{:S(2)}) collective-permute-start(bf16[32,4224]{1,0:T(8,128)(2,1)S(1)} %copy-done.26), channel_id=1, source_target_pairs={{0,2},{1,3},{2,4},{3,5},{4,6},{5,7},{6,0},{7,1},{8,10},{9,11},{10,... | collective-permute-start | bytes 811016 | tf_op jit(solution)/shard_map/ppermute | solution.py:346
  44.6 214.7 %collective-permute-start.2 = (bf16[32,4224]{1,0:T(8,128)(2,1)S(1)}, bf16[32,4224]{1,0:T(8,128)(2,1)S(1)}, u32[]{:S(2)}, u32[]{:S(2)}) collective-permute-start(bf16[32,4224]{1,0:T(8,128)(2,1)S(1)} %copy-done.25), channel_id=1, source_target_pairs={{0,3},{1,4},{2,5},{3,6},{4,7},{5,0},{6,1},{7,2},{8,11},{9,12},{10,... | collective-permute-start | bytes 811016 | tf_op jit(solution)/shard_map/ppermute | solution.py:346
  47.8 222.7 %collective-permute-start.3 = (bf16[32,4224]{1,0:T(8,128)(2,1)S(1)}, bf16[32,4224]{1,0:T(8,128)(2,1)S(1)}, u32[]{:S(2)}, u32[]{:S(2)}) collective-permute-start(bf16[32,4224]{1,0:T(8,128)(2,1)S(1)} %copy-done.24), channel_id=1, source_target_pairs={{0,4},{1,5},{2,6},{3,7},{4,0},{5,1},{6,2},{7,3},{8,12},{9,13},{10,... | collective-permute-start | bytes 811016 | tf_op jit(solution)/shard_map/ppermute | solution.py:346
  48.8 221.7 %collective-permute-start.4 = (bf16[32,4224]{1,0:T(8,128)(2,1)S(1)}, bf16[32,4224]{1,0:T(8,128)(2,1)S(1)}, u32[]{:S(2)}, u32[]{:S(2)}) collective-permute-start(bf16[32,4224]{1,0:T(8,128)(2,1)S(1)} %copy-done.23), channel_id=1, source_target_pairs={{0,5},{1,6},{2,7},{3,0},{4,1},{5,2},{6,3},{7,4},{8,13},{9,14},{10,... | collective-permute-start | bytes 811016 | tf_op jit(solution)/shard_map/ppermute | solution.py:346
  228.3 42.3 %collective-permute-start.5 = (bf16[32,4224]{1,0:T(8,128)(2,1)S(1)}, bf16[32,4224]{1,0:T(8,128)(2,1)S(1)}, u32[]{:S(2)}, u32[]{:S(2)}) collective-permute-start(bf16[32,4224]{1,0:T(8,128)(2,1)S(1)} %copy-done.22), channel_id=1, source_target_pairs={{0,6},{1,7},{2,0},{3,1},{4,2},{5,3},{6,4},{7,5},{8,14},{9,15},{10,... | collective-permute-start | bytes 811016 | tf_op jit(solution)/shard_map/ppermute | solution.py:346
  238.5 32.1 %collective-permute-start.6 = (bf16[32,4224]{1,0:T(8,128)(2,1)S(1)}, bf16[32,4224]{1,0:T(8,128)(2,1)S(1)}, u32[]{:S(2)}, u32[]{:S(2)}) collective-permute-start(bf16[32,4224]{1,0:T(8,128)(2,1)S(1)} %copy-done.21), channel_id=1, source_target_pairs={{0,7},{1,0},{2,1},{3,2},{4,3},{5,4},{6,5},{7,6},{8,15},{9,8},{10,9... | collective-permute-start | bytes 811016 | tf_op jit(solution)/shard_map/ppermute | solution.py:346
  277.6 19.5 %collective-permute-start.7 = (bf16[32,4224]{1,0:T(8,128)(2,1)}, bf16[32,4224]{1,0:T(8,128)(2,1)S(1)}, u32[]{:S(2)}, u32[]{:S(2)}) collective-permute-start(bf16[32,4224]{1,0:T(8,128)(2,1)} %get-tuple-element.87), channel_id=1, source_target_pairs={{0,8},{1,9},{2,10},{3,11},{4,12},{5,13},{6,14},{7,15},{8,16},{9,17... | collective-permute-start | bytes 811016 | tf_op jit(solution)/shard_map/ppermute | solution.py:391
  277.7 19.4 %collective-permute-start.8 = (bf16[32,4224]{1,0:T(8,128)(2,1)}, bf16[32,4224]{1,0:T(8,128)(2,1)S(1)}, u32[]{:S(2)}, u32[]{:S(2)}) collective-permute-start(bf16[32,4224]{1,0:T(8,128)(2,1)} %get-tuple-element.88), channel_id=1, source_target_pairs={{0,16},{1,17},{2,18},{3,19},{4,20},{5,21},{6,22},{7,23},{8,24},{9,... | collective-permute-start | bytes 811016 | tf_op jit(solution)/shard_map/ppermute | solution.py:391
  278.0 19.2 %collective-permute-start.9 = (bf16[32,4224]{1,0:T(8,128)(2,1)}, bf16[32,4224]{1,0:T(8,128)(2,1)S(1)}, u32[]{:S(2)}, u32[]{:S(2)}) collective-permute-start(bf16[32,4224]{1,0:T(8,128)(2,1)} %get-tuple-element.89), channel_id=1, source_target_pairs={{0,24},{1,25},{2,26},{3,27},{4,28},{5,29},{6,30},{7,31},{8,0},{9,1... | collective-permute-start | bytes 811016 | tf_op jit(solution)/shard_map/ppermute | solution.py:391
  280.4 17.0 %collective-permute-start.10 = (bf16[32,4224]{1,0:T(8,128)(2,1)}, bf16[32,4224]{1,0:T(8,128)(2,1)S(1)}, u32[]{:S(2)}, u32[]{:S(2)}) collective-permute-start(bf16[32,4224]{1,0:T(8,128)(2,1)} %get-tuple-element.90), channel_id=1, source_target_pairs={{0,64},{1,65},{2,66},{3,67},{4,68},{5,69},{6,70},{7,71},{8,72},{9,... | collective-permute-start | bytes 811016 | tf_op jit(solution)/shard_map/ppermute | solution.py:391
  280.4 17.1 %collective-permute-start.11 = (bf16[32,4224]{1,0:T(8,128)(2,1)}, bf16[32,4224]{1,0:T(8,128)(2,1)S(1)}, u32[]{:S(2)}, u32[]{:S(2)}) collective-permute-start(bf16[32,4224]{1,0:T(8,128)(2,1)} %get-tuple-element.91), channel_id=1, source_target_pairs={{0,72},{1,73},{2,74},{3,75},{4,76},{5,77},{6,78},{7,79},{8,80},{9,... | collective-permute-start | bytes 811016 | tf_op jit(solution)/shard_map/ppermute | solution.py:391
  297.1 10.2 %collective-permute-start.12 = (bf16[32,4224]{1,0:T(8,128)(2,1)}, bf16[32,4224]{1,0:T(8,128)(2,1)S(1)}, u32[]{:S(2)}, u32[]{:S(2)}) collective-permute-start(bf16[32,4224]{1,0:T(8,128)(2,1)} %get-tuple-element.92), channel_id=1, source_target_pairs={{0,80},{1,81},{2,82},{3,83},{4,84},{5,85},{6,86},{7,87},{8,88},{9,... | collective-permute-start | bytes 811016 | tf_op jit(solution)/shard_map/ppermute | solution.py:391
  297.1 35.6 %collective-permute-start.13 = (bf16[32,4224]{1,0:T(8,128)(2,1)}, bf16[32,4224]{1,0:T(8,128)(2,1)S(1)}, u32[]{:S(2)}, u32[]{:S(2)}) collective-permute-start(bf16[32,4224]{1,0:T(8,128)(2,1)} %get-tuple-element.93), channel_id=1, source_target_pairs={{0,88},{1,89},{2,90},{3,91},{4,92},{5,93},{6,94},{7,95},{8,64},{9,... | collective-permute-start | bytes 811016 | tf_op jit(solution)/shard_map/ppermute | solution.py:391
  297.2 35.5 %collective-permute-start.14 = (bf16[32,4224]{1,0:T(8,128)(2,1)}, bf16[32,4224]{1,0:T(8,128)(2,1)S(1)}, u32[]{:S(2)}, u32[]{:S(2)}) collective-permute-start(bf16[32,4224]{1,0:T(8,128)(2,1)} %get-tuple-element.94), channel_id=1, source_target_pairs={{0,128},{1,129},{2,130},{3,131},{4,132},{5,133},{6,134},{7,135},{8... | collective-permute-start | bytes 811016 | tf_op jit(solution)/shard_map/ppermute | solution.py:391
  297.3 35.5 %collective-permute-start.15 = (bf16[32,4224]{1,0:T(8,128)(2,1)}, bf16[32,4224]{1,0:T(8,128)(2,1)S(1)}, u32[]{:S(2)}, u32[]{:S(2)}) collective-permute-start(bf16[32,4224]{1,0:T(8,128)(2,1)} %get-tuple-element.95), channel_id=1, source_target_pairs={{0,136},{1,137},{2,138},{3,139},{4,140},{5,141},{6,142},{7,143},{8... | collective-permute-start | bytes 811016 | tf_op jit(solution)/shard_map/ppermute | solution.py:391
  297.4 39.0 %collective-permute-start.16 = (bf16[32,4224]{1,0:T(8,128)(2,1)}, bf16[32,4224]{1,0:T(8,128)(2,1)S(1)}, u32[]{:S(2)}, u32[]{:S(2)}) collective-permute-start(bf16[32,4224]{1,0:T(8,128)(2,1)} %get-tuple-element.96), channel_id=1, source_target_pairs={{0,144},{1,145},{2,146},{3,147},{4,148},{5,149},{6,150},{7,151},{8... | collective-permute-start | bytes 811016 | tf_op jit(solution)/shard_map/ppermute | solution.py:391
  307.2 29.2 %collective-permute-start.17 = (bf16[32,4224]{1,0:T(8,128)(2,1)}, bf16[32,4224]{1,0:T(8,128)(2,1)S(1)}, u32[]{:S(2)}, u32[]{:S(2)}) collective-permute-start(bf16[32,4224]{1,0:T(8,128)(2,1)} %get-tuple-element.97), channel_id=1, source_target_pairs={{0,152},{1,153},{2,154},{3,155},{4,156},{5,157},{6,158},{7,159},{8... | collective-permute-start | bytes 811016 | tf_op jit(solution)/shard_map/ppermute | solution.py:391
  332.7 5.5 %collective-permute-start.18 = (bf16[32,4224]{1,0:T(8,128)(2,1)}, bf16[32,4224]{1,0:T(8,128)(2,1)S(1)}, u32[]{:S(2)}, u32[]{:S(2)}) collective-permute-start(bf16[32,4224]{1,0:T(8,128)(2,1)} %get-tuple-element.98), channel_id=1, source_target_pairs={{0,192},{1,193},{2,194},{3,195},{4,196},{5,197},{6,198},{7,199},{8... | collective-permute-start | bytes 811016 | tf_op jit(solution)/shard_map/ppermute | solution.py:391
  332.7 11.7 %collective-permute-start.19 = (bf16[32,4224]{1,0:T(8,128)(2,1)}, bf16[32,4224]{1,0:T(8,128)(2,1)S(1)}, u32[]{:S(2)}, u32[]{:S(2)}) collective-permute-start(bf16[32,4224]{1,0:T(8,128)(2,1)} %get-tuple-element.99), channel_id=1, source_target_pairs={{0,200},{1,201},{2,202},{3,203},{4,204},{5,205},{6,206},{7,207},{8... | collective-permute-start | bytes 811016 | tf_op jit(solution)/shard_map/ppermute | solution.py:391
  332.9 15.4 %collective-permute-start.20 = (bf16[32,4224]{1,0:T(8,128)(2,1)}, bf16[32,4224]{1,0:T(8,128)(2,1)}, u32[]{:S(2)}, u32[]{:S(2)}) collective-permute-start(bf16[32,4224]{1,0:T(8,128)(2,1)} %get-tuple-element.100), channel_id=1, source_target_pairs={{0,208},{1,209},{2,210},{3,211},{4,212},{5,213},{6,214},{7,215},{8... | collective-permute-start | bytes 811016 | tf_op jit(solution)/shard_map/ppermute | solution.py:391
  336.5 22.7 %collective-permute-start.21 = (bf16[32,4224]{1,0:T(8,128)(2,1)}, bf16[32,4224]{1,0:T(8,128)(2,1)}, u32[]{:S(2)}, u32[]{:S(2)}) collective-permute-start(bf16[32,4224]{1,0:T(8,128)(2,1)} %get-tuple-element.101), channel_id=1, source_target_pairs={{0,216},{1,217},{2,218},{3,219},{4,220},{5,221},{6,222},{7,223},{8... | collective-permute-start | bytes 811016 | tf_op jit(solution)/shard_map/ppermute | solution.py:391
  363.4 8.0 %collective-permute-start.22 = (bf16[256,4224]{1,0:T(8,128)(2,1)}, bf16[256,4224]{1,0:T(8,128)(2,1)S(1)}, u32[]{:S(2)}, u32[]{:S(2)}) collective-permute-start(bf16[256,4224]{1,0:T(8,128)(2,1)} %stack.1), channel_id=1, source_target_pairs={{0,32},{1,33},{2,34},{3,35},{4,36},{5,37},{6,38},{7,39},{8,40},{9,... | collective-permute-start | bytes 6488072 | tf_op jit(solution)/shard_map/ppermute | solution.py:401
  (28 other events, 1137.6 us)
where the time goes:
time: 394 us; the launch traced here: 392 us
  waiting for transfers between devices  283 us (72%)
  starting transfers between devices  53.2 us (14%)
  Pallas kernels  51.3 us (13%)
    ppermute x7, waiting for transfers between devices, local(): lax.ppermute(first[d], axes, shifted(0, 0, 0, d))  214 us
    ppermute x15, waiting for transfers between devices, local(): lax.ppermute(second[e], axes, shifted(e // YS, 0, e % YS, 0))  64.9 us
    all_to_all x1, starting transfers between devices, direct(): sent = lax.all_to_all(sent, axes, split_axis=0, concat_axis=0, tiled=True)  16.7 us
    ppermute x15, starting transfers between devices, local(): lax.ppermute(second[e], axes, shifted(e // YS, 0, e % YS, 0))  16.5 us
    ppermute x7, starting transfers between devices, local(): lax.ppermute(first[d], axes, shifted(0, 0, 0, d))  16.2 us
    pallas_call x1, Pallas kernels, direct(): pl.pallas_call(functools.partial(direct_kernel, kind=kind), out_shape=jax...  14.6 us
    pallas_call x1, Pallas kernels, finish(): pl.pallas_call(functools.partial(finish_kernel, tiled=len(packed)), out_s...  13.2 us
  transfers between devices with their start and end apart: 24, of which 11 were waited for; matrix products, arithmetic and copies ran while one was open for 0% of the time, Pallas kernels for 4%

commit v1 on v0

--- a/solution.py
+++ b/solution.py
@@ -113,12 +113,26 @@
 
 def first_kernel(cid, rid, clen, rlen, clogp, rlogp, ref, cg, rg, *refs, row_count):
     outs = refs[:ZS]
-    plan, weight, note, pick = refs[ZS:]
+    plan, weight, note, pick, rows, arrival = refs[ZS:]
     step = pl.program_id(0)
     last = pl.num_programs(0) - 1
+    half = cg.shape[1]
+    few = rows.shape[0]
+
+    def fetches(n):
+        columns = pl.ds(n * WIDE, WIDE)
+        return [
+            pltpu.make_async_copy(
+                grads.at[0, :, columns], rows.at[n, pl.ds(i * half, half)], arrival.at[n, i]
+            )
+            for i, grads in enumerate((cg, rg))
+        ]
 
     @pl.when(step == 0)
     def _():
+        for n in range(few):
+            for fetch in fetches(n):
+                fetch.start()
         route(cid, rid, plan, note, row_count)
         weight[...] = jnp.broadcast_to(
             pair_weight(clen, rlen, clogp, rlogp, ref), weight.shape
@@ -127,9 +141,11 @@
 
     @pl.when(step < last)
     def _():
-        half = cg.shape[1]
+        for fetch in fetches(step):
+            fetch.wait()
         scale = weight[0:1, 0:1]
-        moved = dot(pick[:, :half], cg[0]) * -scale + dot(pick[:, half:], rg[0]) * scale
+        moved = dot(pick[:, :half], rows[step, :half]) * -scale
+        moved += dot(pick[:, half:], rows[step, half:]) * scale
         moved = moved.astype(bf16)
         for d in range(ZS):
             outs[d][...] = moved[d * LIMIT : d * LIMIT + LIMIT]
@@ -148,12 +164,12 @@
         pick[...] = onehot(iota(pick.shape, 0) == plan[kind : kind + 1])
 
     weighted(weight, cg, rg, rows)
-    width = out.shape[1]
+    width = out.shape[2]
     slots = pick.shape[0]
     moved = dot(pick[...], rows[...])
     for u in range(UNITS):
         wide[pl.ds(u, slots, stride=UNITS), :] = moved[:, u * width : (u + 1) * width]
-    out[...] = wide[...].astype(bf16)
+    out[...] = wide[...].astype(bf16).reshape(out.shape)
 
 
 def turned(turn, swap, place):
@@ -264,32 +280,49 @@
     labels = refs[: tiled + 1]
     packed = refs[tiled + 1 : 2 * tiled + 1]
     rest = refs[2 * tiled + 1]
-    out, pick, *scratch = refs[2 * tiled + 2 :]
+    out, pick, *scratch = refs[2 * tiled + 2 : 2 * tiled + 8]
+    *blocks, others, arrival = refs[2 * tiled + 8 :]
     step = pl.program_id(0)
-    half = CHUNK
+
+    def fetches(n):
+        pairs = []
+        for source, block in zip(packed, blocks):
+            tall = block.shape[2]
+            pairs.append((source.at[:, pl.ds(n * tall, tall)], block.at[n]))
+        pairs.append((rest.at[:, pl.ds(n * STEP, STEP)], others.at[n]))
+        return [
+            pltpu.make_async_copy(source, target, arrival.at[n, i])
+            for i, (source, target) in enumerate(pairs)
+        ]
 
     @pl.when(step == 0)
     def _():
+        for n in range(others.shape[0]):
+            for fetch in fetches(n):
+                fetch.start()
         start = 0
         for label in labels:
             size = label.shape[1]
-            block = pick.at[:, start : start + size]
-            block[...] = onehot(iota(block.shape, 0) == label[...])
+            part = pick.at[:, start : start + size]
+            part[...] = onehot(iota(part.shape, 0) == label[...])
             start += size
 
-    total = dot(pick[:, -rest.shape[0] :], rest[...])
+    for fetch in fetches(step):
+        fetch.wait()
+    total = dot(pick[:, -rest.shape[0] :], others[step])
     start = 0
-    for block in packed:
-        width = block.shape[1]
-        for first in range(0, block.shape[0] // UNITS, half):
-            wide, rows = scratch[2 * (start // half % 2) : 2 * (start // half % 2) + 2]
-            wide[...] = block[first * UNITS : (first + half) * UNITS].astype(f32)
+    for block in blocks:
+        _, count, tall, width = block.shape
+        piece = CHUNK * UNITS // tall
+        for first in range(0, count, piece):
+            side = 2 * (start // CHUNK % 2)
+            wide, rows = scratch[side : side + 2]
+            wide[...] = block[step, first : first + piece].astype(f32).reshape(wide.shape)
             for u in range(UNITS):
-                rows[:, u * width : (u + 1) * width] = wide[
-                    pl.ds(u, half, stride=UNITS), :
-                ].astype(bf16)
-            total += dot(pick[:, start : start + half], rows[...])
-            start += half
+                unit = wide[pl.ds(u, CHUNK, stride=UNITS), :].astype(bf16)
+                rows[:, u * width : (u + 1) * width] = unit
+            total += dot(pick[:, start : start + CHUNK], rows[...])
+            start += CHUNK
     out[...] = total[: out.shape[0]].astype(bf16)
 
 
@@ -324,7 +357,6 @@
     padded = (row_count + 15) // 16 * 16
 
     few = features // WIDE
-    part = pl.BlockSpec((1, length, WIDE), lambda n: (0, 0, jnp.minimum(n, few - 1)))
     *first, plan, weight = pl.pallas_call(
         functools.partial(first_kernel, row_count=row_count),
         out_shape=[jax.ShapeDtypeStruct((LIMIT, columns), bf16)] * ZS
@@ -333,12 +365,14 @@
         in_specs=[whole(1, length)] * 2
         + [smem] * 2
         + [whole(1, length)] * 2
-        + [smem, part, part],
+        + [smem] + [pl.BlockSpec(memory_space=pl.ANY)] * 2,
         out_specs=[pl.BlockSpec((LIMIT, WIDE), lambda n: (0, n))] * ZS
         + [whole(8, tokens), whole(8, 128)],
         scratch_shapes=[
             pltpu.VMEM((owners, NOTE), bf16),
             pltpu.VMEM((ZS * LIMIT, tokens), bf16),
+            pltpu.VMEM((few, tokens, WIDE), bf16),
+            pltpu.SemaphoreType.DMA((few, 2)),
         ],
         name="first",
     )(cid, rid, clen, rlen, clogp, rlogp, ref.reshape(2), cg, rg)
@@ -350,7 +384,7 @@
         slots = owners * count
         sent = pl.pallas_call(
             functools.partial(direct_kernel, kind=kind),
-            out_shape=jax.ShapeDtypeStruct((slots * UNITS, features // UNITS), bf16),
+            out_shape=jax.ShapeDtypeStruct((owners, steps * count * UNITS, width), bf16),
             grid=(steps,),
             in_specs=[
                 whole(8, tokens),
@@ -358,7 +392,7 @@
                 pl.BlockSpec((1, length, STEP), lambda n: (0, 0, n)),
                 pl.BlockSpec((1, length, STEP), lambda n: (0, 0, n)),
             ],
-            out_specs=pl.BlockSpec((slots * UNITS, width), lambda n: (0, n)),
+            out_specs=pl.BlockSpec((owners, count * UNITS, width), lambda n: (0, n, 0)),
             scratch_shapes=[
                 pltpu.VMEM((tokens, STEP), bf16),
                 pltpu.VMEM((slots, tokens), bf16),
@@ -366,9 +400,7 @@
             ],
             name="direct",
         )(plan, weight, cg, rg)
-        sent = sent.reshape(owners, count * UNITS, features // UNITS)
-        sent = lax.all_to_all(sent, axes, split_axis=0, concat_axis=0, tiled=True)
-        return sent.reshape(slots * UNITS, features // UNITS)
+        return lax.all_to_all(sent, axes, split_axis=0, concat_axis=0, tiled=True)
 
     arrived = direct(0, DIRECT)
 
@@ -431,15 +463,22 @@
             out_shape=jax.ShapeDtypeStruct((row_count, features), bf16),
             grid=(steps,),
             in_specs=[whole(*label.shape) for label in labels]
-            + [pl.BlockSpec((block.shape[0], width), lambda n: (0, n)) for block in packed]
-            + [pl.BlockSpec((PLANE * each, STEP), lambda n: (0, n))],
+            + [pl.BlockSpec(memory_space=pl.ANY)] * (len(packed) + 1),
             out_specs=pl.BlockSpec((row_count, STEP), lambda n: (0, n)),
             scratch_shapes=[pltpu.VMEM((padded, count), bf16)]
             + [
                 pltpu.VMEM((CHUNK * UNITS, width), f32),
                 pltpu.VMEM((CHUNK, STEP), bf16),
             ]
-            * 2,
+            * 2
+            + [
+                pltpu.VMEM((steps, owners, block.shape[1] // steps, width), bf16)
+                for block in packed
+            ]
+            + [
+                pltpu.VMEM((steps, PLANE * each, STEP), bf16),
+                pltpu.SemaphoreType.DMA((steps, len(packed) + 1)),
+            ],
             name="finish",
         )(*labels, *packed, rest)
 

time: 394 us -> 392 us (level)
  no operation moved by 1% of the time
where the time goes in v1:
time: 392 us; the launch traced here: 391 us
  waiting for transfers between devices  283 us (72%)
  starting transfers between devices  53.2 us (14%)
  Pallas kernels  49.4 us (13%)
    ppermute x7, waiting for transfers between devices, local(): lax.ppermute(first[d], axes, shifted(0, 0, 0, d))  214 us
    ppermute x15, waiting for transfers between devices, local(): lax.ppermute(second[e], axes, shifted(e // YS, 0, e % YS, 0))  64.9 us
    all_to_all x1, starting transfers between devices, direct(): return lax.all_to_all(sent, axes, split_axis=0, concat_axis=0, tiled=True)  16.7 us
    ppermute x15, starting transfers between devices, local(): lax.ppermute(second[e], axes, shifted(e // YS, 0, e % YS, 0))  16.5 us
    ppermute x7, starting transfers between devices, local(): lax.ppermute(first[d], axes, shifted(0, 0, 0, d))  16.2 us
    pallas_call x1, Pallas kernels, direct(): pl.pallas_call(functools.partial(direct_kernel, kind=kind), out_shape=jax...  14.5 us
    pallas_call x1, Pallas kernels, finish(): pl.pallas_call(functools.partial(finish_kernel, tiled=len(packed)), out_s...  11.7 us
  transfers between devices with their start and end apart: 24, of which 11 were waited for; matrix products, arithmetic and copies ran while one was open for 0% of the time, Pallas kernels for 4%

profile of v1, /device:TPU:1, one launch (start us, length us, event | category | flops | bytes accessed | tf_op | source)
XLA Modules:
  0.0 390.7 jit_solution(10511470586845798368)
XLA Ops:
  1.3 7.5 %first.1 = (bf16[32,4224]{1,0:T(8,128)(2,1)}, bf16[32,4224]{1,0:T(8,128)(2,1)}, bf16[32,4224]{1,0:T(8,128)(2,1)}, bf16[32,4224]{1,0:T(8,128)(2,1)}, bf16[32,4224...) custom-call(s32[1,512]{1,0:T(1,128)} %cid.1, ...), custom_call_target="tpu_custom_call" | custom-call | tf_op jit(solution)/shard_map/first/pallas_call | solution.py:360
  8.8 14.5 %direct.3 = bf16[256,128,128]{2,1,0:T(8,128)(2,1)} custom-call(s32[8,1024]{1,0:T(8,128)S(1)} %get-tuple-element.105.plan, f32[8,128]{1,0:T(8,128)S(1)} %get-tuple-element.106.weight, bf16[1,512,4096]{2,1,0:T(8,128)(2,1)} %cg.3, bf16[1,512,4096]{2,1,0:T(8,128)(2,1)} %rg.3), custom_call_target="tpu_custom_call" | custom-call | tf_op jit(solution)/shard_map/direct/pallas_call | solution.py:385
  23.4 16.7 %all-to-all-start.1 = ((bf16[256,128,128]{2,1,0:T(8,128)(2,1)}), bf16[256,128,128]{2,1,0:T(8,128)(2,1)}, u32[]{:S(2)}, u32[]{:S(2)}) async-start(bf16[256,128,128]{2,1,0:T(8,128)(2,1)} %direct.3), calls=%async_computation.1 | async-start | bytes 16777216 | tf_op jit(solution)/shard_map/all_to_all | solution.py:403
  41.6 2.6 collective-permute-start.1
  44.2 3.2 collective-permute-start.2
  48.4 3.7 collective-permute-start.4
  52.2 175.7 %collective-permute-done.refs_1_.refs_9_ = bf16[32,4224]{1,0:T(8,128)(2,1)S(1)} collective-permute-done((bf16[32,4224]{1,0:T(8,128)(2,1)S(1)}, bf16[32,4224]{1,0:T(8,128)(2,1)S(1)}, u32[]{:S(2)}, u32[]{:S(2)}) %collective-permute-start) | collective-permute-done | bytes 270368 | tf_op jit(solution)/shard_map/ppermute | solution.py:380
  229.7 8.4 %collective-permute-done.1.refs_2_.refs_10_ = bf16[32,4224]{1,0:T(8,128)(2,1)S(1)} collective-permute-done((bf16[32,4224]{1,0:T(8,128)(2,1)S(1)}, bf16[32,4224]{1,0:T(8,128)(2,1)S(1)}, u32[]{:S(2)}, u32[]{:S(2)}) %collective-permute-start.1) | collective-permute-done | bytes 270368 | tf_op jit(solution)/shard_map/ppermute | solution.py:380
  240.4 18.6 %collective-permute-done.2.refs_3_.refs_11_ = bf16[32,4224]{1,0:T(8,128)(2,1)S(1)} collective-permute-done((bf16[32,4224]{1,0:T(8,128)(2,1)S(1)}, bf16[32,4224]{1,0:T(8,128)(2,1)S(1)}, u32[]{:S(2)}, u32[]{:S(2)}) %collective-permute-start.2) | collective-permute-done | bytes 270368 | tf_op jit(solution)/shard_map/ppermute | solution.py:380
  258.9 11.2 %collective-permute-done.3.refs_4_.refs_12_ = bf16[32,4224]{1,0:T(8,128)(2,1)S(1)} collective-permute-done((bf16[32,4224]{1,0:T(8,128)(2,1)S(1)}, bf16[32,4224]{1,0:T(8,128)(2,1)S(1)}, u32[]{:S(2)}, u32[]{:S(2)}) %collective-permute-start.3) | collective-permute-done | bytes 270368 | tf_op jit(solution)/shard_map/ppermute | solution.py:380
  271.2 6.0 %second.1 = (bf16[32,4224]{1,0:T(8,128)(2,1)}, bf16[32,4224]{1,0:T(8,128)(2,1)}, bf16[32,4224]{1,0:T(8,128)(2,1)}, bf16[32,4224]{1,0:T(8,128)(2,1)}, bf16[32,422...) custom-call(bf16[32,4224]{1,0:T(8,128)(2,1)} %get-tuple-element.78.r, ...), custom_call_target="tpu_custom_call" | custom-call | tf_op jit(solution)/shard_map/second/pallas_call | solution.py:410
  280.0 16.7 %collective-permute-done.7.refs_1_.refs_18_ = bf16[32,4224]{1,0:T(8,128)(2,1)S(1)} collective-permute-done((bf16[32,4224]{1,0:T(8,128)(2,1)}, bf16[32,4224]{1,0:T(8,128)(2,1)S(1)}, u32[]{:S(2)}, u32[]{:S(2)}) %collective-permute-start.7) | collective-permute-done | bytes 270368 | tf_op jit(solution)/shard_map/ppermute | solution.py:423
  297.1 9.8 %collective-permute-start.16 = (bf16[32,4224]{1,0:T(8,128)(2,1)}, bf16[32,4224]{1,0:T(8,128)(2,1)S(1)}, u32[]{:S(2)}, u32[]{:S(2)}) collective-permute-start(bf16[32,4224]{1,0:T(8,128)(2,1)} %get-tuple-element.96), channel_id=1, source_target_pairs={{0,144},{1,145},{2,146},{3,147},{4,148},{5,149},{6,150},{7,151},{8... | collective-permute-start | bytes 811016 | tf_op jit(solution)/shard_map/ppermute | solution.py:423
  306.9 25.5 %collective-permute-done.13.refs_7_.refs_24_ = bf16[32,4224]{1,0:T(8,128)(2,1)S(1)} collective-permute-done((bf16[32,4224]{1,0:T(8,128)(2,1)}, bf16[32,4224]{1,0:T(8,128)(2,1)S(1)}, u32[]{:S(2)}, u32[]{:S(2)}) %collective-permute-start.13) | collective-permute-done | bytes 270368 | tf_op jit(solution)/shard_map/ppermute | solution.py:423
  332.5 3.6 collective-permute-start.20
  337.9 6.2 %collective-permute-done.19.refs_13_.refs_30_ = bf16[32,4224]{1,0:T(8,128)(2,1)S(1)} collective-permute-done((bf16[32,4224]{1,0:T(8,128)(2,1)}, bf16[32,4224]{1,0:T(8,128)(2,1)S(1)}, u32[]{:S(2)}, u32[]{:S(2)}) %collective-permute-start.19) | collective-permute-done | bytes 270368 | tf_op jit(solution)/shard_map/ppermute | solution.py:423
  344.1 3.8 collective-permute-done.20.refs_14_.refs_31_
  347.8 11.0 %collective-permute-done.21.refs_15_.refs_32_ = bf16[32,4224]{1,0:T(8,128)(2,1)} collective-permute-done((bf16[32,4224]{1,0:T(8,128)(2,1)}, bf16[32,4224]{1,0:T(8,128)(2,1)}, u32[]{:S(2)}, u32[]{:S(2)}) %collective-permute-start.21) | collective-permute-done | bytes 270368 | tf_op jit(solution)/shard_map/ppermute | solution.py:423
  358.9 4.1 %stack.1 = bf16[256,4224]{1,0:T(8,128)(2,1)} custom-call(bf16[32,4224]{1,0:T(8,128)(2,1)} %get-tuple-element.86.refs_0_.refs_17_, bf16[32,4224]{1,0:T(8,128)(2,1)} %copy-done.1, bf16[32,4224]{1,0:T(8,128)(2,1)} %copy-done.2, bf16[32,4224]{1,0:T(8,128)(2,1)} %copy-done.3, bf16[32,4224]{1,0:T(8,128)(2,1)} %copy-done.4, bf16[32,4224]{1,0:T(8,128)(2,1)} %copy-done.5, ...), custom_call_target="tpu_custom_call" | custom-call | tf_op jit(solution)/shard_map/stack/pallas_call | solution.py:425
  363.0 3.9 collective-permute-start.22
  366.9 4.1 %collective-permute-done.22.refs_16_.refs_33_ = bf16[256,4224]{1,0:T(8,128)(2,1)S(1)} collective-permute-done((bf16[256,4224]{1,0:T(8,128)(2,1)}, bf16[256,4224]{1,0:T(8,128)(2,1)S(1)}, u32[]{:S(2)}, u32[]{:S(2)}) %collective-permute-start.22) | collective-permute-done | bytes 2162720 | tf_op jit(solution)/shard_map/ppermute | solution.py:433
  372.4 5.6 %collect.1 = (bf16[512,4096]{1,0:T(8,128)(2,1)}, s32[1,1024]{1,0:T(1,128)S(1)}, s32[1,512]{1,0:T(1,128)S(1)}, s32[1,512]{1,0:T(1,128)S(1)}, s32[1]{0:T(128)}) custom-call(bf16[32,4224]{1,0:T(8,128)(2,1)} %get-tuple-element.86.refs_0_.refs_17_, bf16[32,4224]{1,0:T(8,128)(2,1)} %copy-done.1, bf16[32,4224]{1,0:T(8,128)(2,1)} %copy-done.2, ...), custom_call_target="tpu_custom_call" | custom-call | tf_op jit(solution)/shard_map/collect/pallas_call | solution.py:435
  378.6 11.9 %conditional.1 = (bf16[501,4096]{1,0:T(8,128)(2,1)}) conditional(s32[]{:T(128)} %bitcast.1, (s32[1,1024]{1,0:T(1,128)S(1)}, s32[1,512]{1,0:T(1,128)S(1)}, bf16[256,128,128]{2,1,0:T(8,128)(2,1)}, bf16[512,4096]{1,0:T(8,128)(2,1)}) %tuple.11, (s32[8,1024]{1,0:T(8,128)S(1)}, f32[8,128]{1,0:T(8,128)S(1)}, bf16[1,512,4096]{2,1,0:T(8,128)(2,1)}, ...), branch_computations={%region_0.0_spmd, %region_1.0_spmd} | conditional | bytes 8388616 | solution.py:485
  378.8 11.7 %finish.2 = bf16[501,4096]{1,0:T(8,128)(2,1)} custom-call(s32[1,1024]{1,0:T(1,128)S(1)} %get-tuple-element.34.refs_0_, s32[1,512]{1,0:T(1,128)S(1)} %get-tuple-element.35.refs_1_, bf16[256,128,128]{2,1,0:T(8,128)(2,1)} %get-tuple-element.36.refs_2_, bf16[512,4096]{1,0:T(8,128)(2,1)} %get-tuple-element.37.refs_3_), custom_call_target="tpu_custom_call" | custom-call | tf_op jit(solution)/shard_map/cond/branch_0_fun/finish/pallas_call | solution.py:461
  (87 shorter events, 13.9 us)
Async XLA Ops:
  23.4 355.2 %all-to-all-start.1 = ((bf16[256,128,128]{2,1,0:T(8,128)(2,1)}), bf16[256,128,128]{2,1,0:T(8,128)(2,1)}, u32[]{:S(2)}, u32[]{:S(2)}) async-start(bf16[256,128,128]{2,1,0:T(8,128)(2,1)} %direct.3), calls=%async_computation.1 | async-start | bytes 16777216 | tf_op jit(solution)/shard_map/all_to_all | solution.py:403
  40.0 187.9 %collective-permute-start = (bf16[32,4224]{1,0:T(8,128)(2,1)S(1)}, bf16[32,4224]{1,0:T(8,128)(2,1)S(1)}, u32[]{:S(2)}, u32[]{:S(2)}) collective-permute-start(bf16[32,4224]{1,0:T(8,128)(2,1)S(1)} %copy-done.27), channel_id=1, source_target_pairs={{0,1},{1,2},{2,3},{3,4},{4,5},{5,6},{6,7},{7,0},{8,9},{9,10},{10,1... | collective-permute-start | bytes 811016 | tf_op jit(solution)/shard_map/ppermute | solution.py:380
  41.6 196.5 %collective-permute-start.1 = (bf16[32,4224]{1,0:T(8,128)(2,1)S(1)}, bf16[32,4224]{1,0:T(8,128)(2,1)S(1)}, u32[]{:S(2)}, u32[]{:S(2)}) collective-permute-start(bf16[32,4224]{1,0:T(8,128)(2,1)S(1)} %copy-done.26), channel_id=1, source_target_pairs={{0,2},{1,3},{2,4},{3,5},{4,6},{5,7},{6,0},{7,1},{8,10},{9,11},{10,... | collective-permute-start | bytes 811016 | tf_op jit(solution)/shard_map/ppermute | solution.py:380
  44.2 214.7 %collective-permute-start.2 = (bf16[32,4224]{1,0:T(8,128)(2,1)S(1)}, bf16[32,4224]{1,0:T(8,128)(2,1)S(1)}, u32[]{:S(2)}, u32[]{:S(2)}) collective-permute-start(bf16[32,4224]{1,0:T(8,128)(2,1)S(1)} %copy-done.25), channel_id=1, source_target_pairs={{0,3},{1,4},{2,5},{3,6},{4,7},{5,0},{6,1},{7,2},{8,11},{9,12},{10,... | collective-permute-start | bytes 811016 | tf_op jit(solution)/shard_map/ppermute | solution.py:380
  47.4 222.7 %collective-permute-start.3 = (bf16[32,4224]{1,0:T(8,128)(2,1)S(1)}, bf16[32,4224]{1,0:T(8,128)(2,1)S(1)}, u32[]{:S(2)}, u32[]{:S(2)}) collective-permute-start(bf16[32,4224]{1,0:T(8,128)(2,1)S(1)} %copy-done.24), channel_id=1, source_target_pairs={{0,4},{1,5},{2,6},{3,7},{4,0},{5,1},{6,2},{7,3},{8,12},{9,13},{10,... | collective-permute-start | bytes 811016 | tf_op jit(solution)/shard_map/ppermute | solution.py:380
  48.4 221.7 %collective-permute-start.4 = (bf16[32,4224]{1,0:T(8,128)(2,1)S(1)}, bf16[32,4224]{1,0:T(8,128)(2,1)S(1)}, u32[]{:S(2)}, u32[]{:S(2)}) collective-permute-start(bf16[32,4224]{1,0:T(8,128)(2,1)S(1)} %copy-done.23), channel_id=1, source_target_pairs={{0,5},{1,6},{2,7},{3,0},{4,1},{5,2},{6,3},{7,4},{8,13},{9,14},{10,... | collective-permute-start | bytes 811016 | tf_op jit(solution)/shard_map/ppermute | solution.py:380
  227.9 42.3 %collective-permute-start.5 = (bf16[32,4224]{1,0:T(8,128)(2,1)S(1)}, bf16[32,4224]{1,0:T(8,128)(2,1)S(1)}, u32[]{:S(2)}, u32[]{:S(2)}) collective-permute-start(bf16[32,4224]{1,0:T(8,128)(2,1)S(1)} %copy-done.22), channel_id=1, source_target_pairs={{0,6},{1,7},{2,0},{3,1},{4,2},{5,3},{6,4},{7,5},{8,14},{9,15},{10,... | collective-permute-start | bytes 811016 | tf_op jit(solution)/shard_map/ppermute | solution.py:380
  238.1 32.1 %collective-permute-start.6 = (bf16[32,4224]{1,0:T(8,128)(2,1)S(1)}, bf16[32,4224]{1,0:T(8,128)(2,1)S(1)}, u32[]{:S(2)}, u32[]{:S(2)}) collective-permute-start(bf16[32,4224]{1,0:T(8,128)(2,1)S(1)} %copy-done.21), channel_id=1, source_target_pairs={{0,7},{1,0},{2,1},{3,2},{4,3},{5,4},{6,5},{7,6},{8,15},{9,8},{10,9... | collective-permute-start | bytes 811016 | tf_op jit(solution)/shard_map/ppermute | solution.py:380
  277.2 19.5 %collective-permute-start.7 = (bf16[32,4224]{1,0:T(8,128)(2,1)}, bf16[32,4224]{1,0:T(8,128)(2,1)S(1)}, u32[]{:S(2)}, u32[]{:S(2)}) collective-permute-start(bf16[32,4224]{1,0:T(8,128)(2,1)} %get-tuple-element.87), channel_id=1, source_target_pairs={{0,8},{1,9},{2,10},{3,11},{4,12},{5,13},{6,14},{7,15},{8,16},{9,17... | collective-permute-start | bytes 811016 | tf_op jit(solution)/shard_map/ppermute | solution.py:423
  277.3 19.4 %collective-permute-start.8 = (bf16[32,4224]{1,0:T(8,128)(2,1)}, bf16[32,4224]{1,0:T(8,128)(2,1)S(1)}, u32[]{:S(2)}, u32[]{:S(2)}) collective-permute-start(bf16[32,4224]{1,0:T(8,128)(2,1)} %get-tuple-element.88), channel_id=1, source_target_pairs={{0,16},{1,17},{2,18},{3,19},{4,20},{5,21},{6,22},{7,23},{8,24},{9,... | collective-permute-start | bytes 811016 | tf_op jit(solution)/shard_map/ppermute | solution.py:423
  277.6 19.2 %collective-permute-start.9 = (bf16[32,4224]{1,0:T(8,128)(2,1)}, bf16[32,4224]{1,0:T(8,128)(2,1)S(1)}, u32[]{:S(2)}, u32[]{:S(2)}) collective-permute-start(bf16[32,4224]{1,0:T(8,128)(2,1)} %get-tuple-element.89), channel_id=1, source_target_pairs={{0,24},{1,25},{2,26},{3,27},{4,28},{5,29},{6,30},{7,31},{8,0},{9,1... | collective-permute-start | bytes 811016 | tf_op jit(solution)/shard_map/ppermute | solution.py:423
  279.9 17.0 %collective-permute-start.10 = (bf16[32,4224]{1,0:T(8,128)(2,1)}, bf16[32,4224]{1,0:T(8,128)(2,1)S(1)}, u32[]{:S(2)}, u32[]{:S(2)}) collective-permute-start(bf16[32,4224]{1,0:T(8,128)(2,1)} %get-tuple-element.90), channel_id=1, source_target_pairs={{0,64},{1,65},{2,66},{3,67},{4,68},{5,69},{6,70},{7,71},{8,72},{9,... | collective-permute-start | bytes 811016 | tf_op jit(solution)/shard_map/ppermute | solution.py:423
  279.9 17.1 %collective-permute-start.11 = (bf16[32,4224]{1,0:T(8,128)(2,1)}, bf16[32,4224]{1,0:T(8,128)(2,1)S(1)}, u32[]{:S(2)}, u32[]{:S(2)}) collective-permute-start(bf16[32,4224]{1,0:T(8,128)(2,1)} %get-tuple-element.91), channel_id=1, source_target_pairs={{0,72},{1,73},{2,74},{3,75},{4,76},{5,77},{6,78},{7,79},{8,80},{9,... | collective-permute-start | bytes 811016 | tf_op jit(solution)/shard_map/ppermute | solution.py:423
  296.7 10.2 %collective-permute-start.12 = (bf16[32,4224]{1,0:T(8,128)(2,1)}, bf16[32,4224]{1,0:T(8,128)(2,1)S(1)}, u32[]{:S(2)}, u32[]{:S(2)}) collective-permute-start(bf16[32,4224]{1,0:T(8,128)(2,1)} %get-tuple-element.92), channel_id=1, source_target_pairs={{0,80},{1,81},{2,82},{3,83},{4,84},{5,85},{6,86},{7,87},{8,88},{9,... | collective-permute-start | bytes 811016 | tf_op jit(solution)/shard_map/ppermute | solution.py:423
  296.7 35.6 %collective-permute-start.13 = (bf16[32,4224]{1,0:T(8,128)(2,1)}, bf16[32,4224]{1,0:T(8,128)(2,1)S(1)}, u32[]{:S(2)}, u32[]{:S(2)}) collective-permute-start(bf16[32,4224]{1,0:T(8,128)(2,1)} %get-tuple-element.93), channel_id=1, source_target_pairs={{0,88},{1,89},{2,90},{3,91},{4,92},{5,93},{6,94},{7,95},{8,64},{9,... | collective-permute-start | bytes 811016 | tf_op jit(solution)/shard_map/ppermute | solution.py:423
  296.8 35.5 %collective-permute-start.14 = (bf16[32,4224]{1,0:T(8,128)(2,1)}, bf16[32,4224]{1,0:T(8,128)(2,1)S(1)}, u32[]{:S(2)}, u32[]{:S(2)}) collective-permute-start(bf16[32,4224]{1,0:T(8,128)(2,1)} %get-tuple-element.94), channel_id=1, source_target_pairs={{0,128},{1,129},{2,130},{3,131},{4,132},{5,133},{6,134},{7,135},{8... | collective-permute-start | bytes 811016 | tf_op jit(solution)/shard_map/ppermute | solution.py:423
  296.9 35.5 %collective-permute-start.15 = (bf16[32,4224]{1,0:T(8,128)(2,1)}, bf16[32,4224]{1,0:T(8,128)(2,1)S(1)}, u32[]{:S(2)}, u32[]{:S(2)}) collective-permute-start(bf16[32,4224]{1,0:T(8,128)(2,1)} %get-tuple-element.95), channel_id=1, source_target_pairs={{0,136},{1,137},{2,138},{3,139},{4,140},{5,141},{6,142},{7,143},{8... | collective-permute-start | bytes 811016 | tf_op jit(solution)/shard_map/ppermute | solution.py:423
  297.1 39.0 %collective-permute-start.16 = (bf16[32,4224]{1,0:T(8,128)(2,1)}, bf16[32,4224]{1,0:T(8,128)(2,1)S(1)}, u32[]{:S(2)}, u32[]{:S(2)}) collective-permute-start(bf16[32,4224]{1,0:T(8,128)(2,1)} %get-tuple-element.96), channel_id=1, source_target_pairs={{0,144},{1,145},{2,146},{3,147},{4,148},{5,149},{6,150},{7,151},{8... | collective-permute-start | bytes 811016 | tf_op jit(solution)/shard_map/ppermute | solution.py:423
  306.9 29.2 %collective-permute-start.17 = (bf16[32,4224]{1,0:T(8,128)(2,1)}, bf16[32,4224]{1,0:T(8,128)(2,1)S(1)}, u32[]{:S(2)}, u32[]{:S(2)}) collective-permute-start(bf16[32,4224]{1,0:T(8,128)(2,1)} %get-tuple-element.97), channel_id=1, source_target_pairs={{0,152},{1,153},{2,154},{3,155},{4,156},{5,157},{6,158},{7,159},{8... | collective-permute-start | bytes 811016 | tf_op jit(solution)/shard_map/ppermute | solution.py:423
  332.3 5.5 %collective-permute-start.18 = (bf16[32,4224]{1,0:T(8,128)(2,1)}, bf16[32,4224]{1,0:T(8,128)(2,1)S(1)}, u32[]{:S(2)}, u32[]{:S(2)}) collective-permute-start(bf16[32,4224]{1,0:T(8,128)(2,1)} %get-tuple-element.98), channel_id=1, source_target_pairs={{0,192},{1,193},{2,194},{3,195},{4,196},{5,197},{6,198},{7,199},{8... | collective-permute-start | bytes 811016 | tf_op jit(solution)/shard_map/ppermute | solution.py:423
  332.4 11.7 %collective-permute-start.19 = (bf16[32,4224]{1,0:T(8,128)(2,1)}, bf16[32,4224]{1,0:T(8,128)(2,1)S(1)}, u32[]{:S(2)}, u32[]{:S(2)}) collective-permute-start(bf16[32,4224]{1,0:T(8,128)(2,1)} %get-tuple-element.99), channel_id=1, source_target_pairs={{0,200},{1,201},{2,202},{3,203},{4,204},{5,205},{6,206},{7,207},{8... | collective-permute-start | bytes 811016 | tf_op jit(solution)/shard_map/ppermute | solution.py:423
  332.5 15.4 %collective-permute-start.20 = (bf16[32,4224]{1,0:T(8,128)(2,1)}, bf16[32,4224]{1,0:T(8,128)(2,1)}, u32[]{:S(2)}, u32[]{:S(2)}) collective-permute-start(bf16[32,4224]{1,0:T(8,128)(2,1)} %get-tuple-element.100), channel_id=1, source_target_pairs={{0,208},{1,209},{2,210},{3,211},{4,212},{5,213},{6,214},{7,215},{8... | collective-permute-start | bytes 811016 | tf_op jit(solution)/shard_map/ppermute | solution.py:423
  336.1 22.7 %collective-permute-start.21 = (bf16[32,4224]{1,0:T(8,128)(2,1)}, bf16[32,4224]{1,0:T(8,128)(2,1)}, u32[]{:S(2)}, u32[]{:S(2)}) collective-permute-start(bf16[32,4224]{1,0:T(8,128)(2,1)} %get-tuple-element.101), channel_id=1, source_target_pairs={{0,216},{1,217},{2,218},{3,219},{4,220},{5,221},{6,222},{7,223},{8... | collective-permute-start | bytes 811016 | tf_op jit(solution)/shard_map/ppermute | solution.py:423
  363.0 8.0 %collective-permute-start.22 = (bf16[256,4224]{1,0:T(8,128)(2,1)}, bf16[256,4224]{1,0:T(8,128)(2,1)S(1)}, u32[]{:S(2)}, u32[]{:S(2)}) collective-permute-start(bf16[256,4224]{1,0:T(8,128)(2,1)} %stack.1), channel_id=1, source_target_pairs={{0,32},{1,33},{2,34},{3,35},{4,36},{5,37},{6,38},{7,39},{8,40},{9,... | collective-permute-start | bytes 6488072 | tf_op jit(solution)/shard_map/ppermute | solution.py:433
  (28 other events, 1137.6 us)

commit v2 on v1

--- a/solution.py
+++ b/solution.py
@@ -22,6 +22,7 @@
 STEP = 512
 WIDE = 1024
 CHUNK = 512
+WAYS = sorted(range(1, ZS), key=lambda d: -min(d, ZS - d))
 TURNS = XS * YS
 
 bf16 = jnp.bfloat16
@@ -97,8 +98,8 @@
 def pair_weight(clen, rlen, clogp, rlogp, ref):
     length = clogp.shape[1]
     positions = iota((1, length), 1)
-    chosen_mask = (positions >= length - clen[0]).astype(f32)
-    rejected_mask = (positions >= length - rlen[0]).astype(f32)
+    chosen_mask = (positions >= length - clen).astype(f32)
+    rejected_mask = (positions >= length - rlen).astype(f32)
     chosen = jnp.sum(chosen_mask * clogp[...], axis=1, keepdims=True)
     rejected = jnp.sum(rejected_mask * rlogp[...], axis=1, keepdims=True)
     margin = BETA * ((chosen - ref[0]) - (rejected - ref[1]))
@@ -111,7 +112,7 @@
     rows[half:] = (weight[0:1, 0:1] * rg[0].astype(f32)).astype(bf16)
 
 
-def first_kernel(cid, rid, clen, rlen, clogp, rlogp, ref, cg, rg, *refs, row_count):
+def first_kernel(cid, rid, lengths, clogp, rlogp, ref, cg, rg, *refs, row_count):
     outs = refs[:ZS]
     plan, weight, note, pick, rows, arrival = refs[ZS:]
     step = pl.program_id(0)
@@ -135,7 +136,7 @@
                 fetch.start()
         route(cid, rid, plan, note, row_count)
         weight[...] = jnp.broadcast_to(
-            pair_weight(clen, rlen, clogp, rlogp, ref), weight.shape
+            pair_weight(lengths[0], lengths[1], clogp, rlogp, ref), weight.shape
         )
         pick[...] = onehot(iota(pick.shape, 0) == plan[1:2])
 
@@ -363,7 +364,7 @@
         + [jax.ShapeDtypeStruct((8, tokens), i32), jax.ShapeDtypeStruct((8, 128), f32)],
         grid=(few + 1,),
         in_specs=[whole(1, length)] * 2
-        + [smem] * 2
+        + [smem]
         + [whole(1, length)] * 2
         + [smem] + [pl.BlockSpec(memory_space=pl.ANY)] * 2,
         out_specs=[pl.BlockSpec((LIMIT, WIDE), lambda n: (0, n))] * ZS
@@ -375,10 +376,19 @@
             pltpu.SemaphoreType.DMA((few, 2)),
         ],
         name="first",
-    )(cid, rid, clen, rlen, clogp, rlogp, ref.reshape(2), cg, rg)
-    hopped = [first[0]] + [
-        lax.ppermute(first[d], axes, shifted(0, 0, 0, d)) for d in range(1, ZS)
-    ]
+    )(
+        cid,
+        rid,
+        jnp.concatenate([clen, rlen]),
+        clogp,
+        rlogp,
+        ref.reshape(2),
+        cg,
+        rg,
+    )
+    hopped = list(first)
+    for d in WAYS:
+        hopped[d] = lax.ppermute(first[d], axes, shifted(0, 0, 0, d))
 
     def direct(kind, count):
         slots = owners * count

time: 392 us -> 392 us (level)
  no operation moved by 1% of the time
where the time goes in v2:
time: 392 us; the launch traced here: 391 us
  waiting for transfers between devices  283 us (72%)
  starting transfers between devices  53.2 us (14%)
  Pallas kernels  49.4 us (13%)
    ppermute x7, waiting for transfers between devices, local(): hopped[d] = lax.ppermute(first[d], axes, shifted(0, 0, 0, d))  214 us
    ppermute x15, waiting for transfers between devices, local(): lax.ppermute(second[e], axes, shifted(e // YS, 0, e % YS, 0))  64.9 us
    all_to_all x1, starting transfers between devices, direct(): return lax.all_to_all(sent, axes, split_axis=0, concat_axis=0, tiled=True)  16.7 us
    ppermute x15, starting transfers between devices, local(): lax.ppermute(second[e], axes, shifted(e // YS, 0, e % YS, 0))  16.5 us
    ppermute x7, starting transfers between devices, local(): hopped[d] = lax.ppermute(first[d], axes, shifted(0, 0, 0, d))  16.2 us
    pallas_call x1, Pallas kernels, direct(): pl.pallas_call(functools.partial(direct_kernel, kind=kind), out_shape=jax...  14.6 us
    pallas_call x1, Pallas kernels, finish(): pl.pallas_call(functools.partial(finish_kernel, tiled=len(packed)), out_s...  11.7 us
  transfers between devices with their start and end apart: 24, of which 11 were waited for; matrix products, arithmetic and copies ran while one was open for 0% of the time, Pallas kernels for 4%

profile of v2, /device:TPU:1, one launch (start us, length us, event | category | flops | bytes accessed | tf_op | source)
XLA Modules:
  0.0 391.3 jit_solution(11419918687892832379)
XLA Ops:
  1.9 7.5 %first.1 = (bf16[32,4224]{1,0:T(8,128)(2,1)}, bf16[32,4224]{1,0:T(8,128)(2,1)}, bf16[32,4224]{1,0:T(8,128)(2,1)}, bf16[32,4224]{1,0:T(8,128)(2,1)}, bf16[32,4224...) custom-call(s32[1,512]{1,0:T(1,128)} %cid.1, ...), custom_call_target="tpu_custom_call" | custom-call | tf_op jit(solution)/shard_map/first/pallas_call | solution.py:361
  9.4 14.6 %direct.3 = bf16[256,128,128]{2,1,0:T(8,128)(2,1)} custom-call(s32[8,1024]{1,0:T(8,128)S(1)} %get-tuple-element.105.plan, f32[8,128]{1,0:T(8,128)S(1)} %get-tuple-element.106.weight, bf16[1,512,4096]{2,1,0:T(8,128)(2,1)} %cg.3, bf16[1,512,4096]{2,1,0:T(8,128)(2,1)} %rg.3), custom_call_target="tpu_custom_call" | custom-call | tf_op jit(solution)/shard_map/direct/pallas_call | solution.py:395
  24.0 16.7 %all-to-all-start.1 = ((bf16[256,128,128]{2,1,0:T(8,128)(2,1)}), bf16[256,128,128]{2,1,0:T(8,128)(2,1)}, u32[]{:S(2)}, u32[]{:S(2)}) async-start(bf16[256,128,128]{2,1,0:T(8,128)(2,1)} %direct.3), calls=%async_computation.1 | async-start | bytes 16777216 | tf_op jit(solution)/shard_map/all_to_all | solution.py:413
  42.2 2.6 collective-permute-start.1
  44.8 3.2 collective-permute-start.2
  49.0 3.7 collective-permute-start.4
  52.8 175.7 %collective-permute-done.refs_1_.refs_9_ = bf16[32,4224]{1,0:T(8,128)(2,1)S(1)} collective-permute-done((bf16[32,4224]{1,0:T(8,128)(2,1)S(1)}, bf16[32,4224]{1,0:T(8,128)(2,1)S(1)}, u32[]{:S(2)}, u32[]{:S(2)}) %collective-permute-start) | collective-permute-done | bytes 270368 | tf_op jit(solution)/shard_map/ppermute | solution.py:391
  230.3 8.4 %collective-permute-done.1.refs_2_.refs_10_ = bf16[32,4224]{1,0:T(8,128)(2,1)S(1)} collective-permute-done((bf16[32,4224]{1,0:T(8,128)(2,1)S(1)}, bf16[32,4224]{1,0:T(8,128)(2,1)S(1)}, u32[]{:S(2)}, u32[]{:S(2)}) %collective-permute-start.1) | collective-permute-done | bytes 270368 | tf_op jit(solution)/shard_map/ppermute | solution.py:391
  241.0 18.6 %collective-permute-done.2.refs_3_.refs_11_ = bf16[32,4224]{1,0:T(8,128)(2,1)S(1)} collective-permute-done((bf16[32,4224]{1,0:T(8,128)(2,1)S(1)}, bf16[32,4224]{1,0:T(8,128)(2,1)S(1)}, u32[]{:S(2)}, u32[]{:S(2)}) %collective-permute-start.2) | collective-permute-done | bytes 270368 | tf_op jit(solution)/shard_map/ppermute | solution.py:391
  259.5 11.2 %collective-permute-done.3.refs_4_.refs_12_ = bf16[32,4224]{1,0:T(8,128)(2,1)S(1)} collective-permute-done((bf16[32,4224]{1,0:T(8,128)(2,1)S(1)}, bf16[32,4224]{1,0:T(8,128)(2,1)S(1)}, u32[]{:S(2)}, u32[]{:S(2)}) %collective-permute-start.3) | collective-permute-done | bytes 270368 | tf_op jit(solution)/shard_map/ppermute | solution.py:391
  271.7 6.0 %second.1 = (bf16[32,4224]{1,0:T(8,128)(2,1)}, bf16[32,4224]{1,0:T(8,128)(2,1)}, bf16[32,4224]{1,0:T(8,128)(2,1)}, bf16[32,4224]{1,0:T(8,128)(2,1)}, bf16[32,422...) custom-call(bf16[32,4224]{1,0:T(8,128)(2,1)} %get-tuple-element.78.r, ...), custom_call_target="tpu_custom_call" | custom-call | tf_op jit(solution)/shard_map/second/pallas_call | solution.py:420
  280.5 16.7 %collective-permute-done.7.refs_1_.refs_18_ = bf16[32,4224]{1,0:T(8,128)(2,1)S(1)} collective-permute-done((bf16[32,4224]{1,0:T(8,128)(2,1)}, bf16[32,4224]{1,0:T(8,128)(2,1)S(1)}, u32[]{:S(2)}, u32[]{:S(2)}) %collective-permute-start.7) | collective-permute-done | bytes 270368 | tf_op jit(solution)/shard_map/ppermute | solution.py:433
  297.6 9.8 %collective-permute-start.16 = (bf16[32,4224]{1,0:T(8,128)(2,1)}, bf16[32,4224]{1,0:T(8,128)(2,1)S(1)}, u32[]{:S(2)}, u32[]{:S(2)}) collective-permute-start(bf16[32,4224]{1,0:T(8,128)(2,1)} %get-tuple-element.96), channel_id=1, source_target_pairs={{0,144},{1,145},{2,146},{3,147},{4,148},{5,149},{6,150},{7,151},{8... | collective-permute-start | bytes 811016 | tf_op jit(solution)/shard_map/ppermute | solution.py:433
  307.4 25.5 %collective-permute-done.13.refs_7_.refs_24_ = bf16[32,4224]{1,0:T(8,128)(2,1)S(1)} collective-permute-done((bf16[32,4224]{1,0:T(8,128)(2,1)}, bf16[32,4224]{1,0:T(8,128)(2,1)S(1)}, u32[]{:S(2)}, u32[]{:S(2)}) %collective-permute-start.13) | collective-permute-done | bytes 270368 | tf_op jit(solution)/shard_map/ppermute | solution.py:433
  333.0 3.6 collective-permute-start.20
  338.4 6.2 %collective-permute-done.19.refs_13_.refs_30_ = bf16[32,4224]{1,0:T(8,128)(2,1)S(1)} collective-permute-done((bf16[32,4224]{1,0:T(8,128)(2,1)}, bf16[32,4224]{1,0:T(8,128)(2,1)S(1)}, u32[]{:S(2)}, u32[]{:S(2)}) %collective-permute-start.19) | collective-permute-done | bytes 270368 | tf_op jit(solution)/shard_map/ppermute | solution.py:433
  344.6 3.8 collective-permute-done.20.refs_14_.refs_31_
  348.4 11.0 %collective-permute-done.21.refs_15_.refs_32_ = bf16[32,4224]{1,0:T(8,128)(2,1)} collective-permute-done((bf16[32,4224]{1,0:T(8,128)(2,1)}, bf16[32,4224]{1,0:T(8,128)(2,1)}, u32[]{:S(2)}, u32[]{:S(2)}) %collective-permute-start.21) | collective-permute-done | bytes 270368 | tf_op jit(solution)/shard_map/ppermute | solution.py:433
  359.5 4.1 %stack.1 = bf16[256,4224]{1,0:T(8,128)(2,1)} custom-call(bf16[32,4224]{1,0:T(8,128)(2,1)} %get-tuple-element.86.refs_0_.refs_17_, bf16[32,4224]{1,0:T(8,128)(2,1)} %copy-done.1, bf16[32,4224]{1,0:T(8,128)(2,1)} %copy-done.2, bf16[32,4224]{1,0:T(8,128)(2,1)} %copy-done.3, bf16[32,4224]{1,0:T(8,128)(2,1)} %copy-done.4, bf16[32,4224]{1,0:T(8,128)(2,1)} %copy-done.5, ...), custom_call_target="tpu_custom_call" | custom-call | tf_op jit(solution)/shard_map/stack/pallas_call | solution.py:435
  363.6 3.9 collective-permute-start.22
  367.5 4.1 %collective-permute-done.22.refs_16_.refs_33_ = bf16[256,4224]{1,0:T(8,128)(2,1)S(1)} collective-permute-done((bf16[256,4224]{1,0:T(8,128)(2,1)}, bf16[256,4224]{1,0:T(8,128)(2,1)S(1)}, u32[]{:S(2)}, u32[]{:S(2)}) %collective-permute-start.22) | collective-permute-done | bytes 2162720 | tf_op jit(solution)/shard_map/ppermute | solution.py:443
  372.9 5.6 %collect.1 = (bf16[512,4096]{1,0:T(8,128)(2,1)}, s32[1,1024]{1,0:T(1,128)S(1)}, s32[1,512]{1,0:T(1,128)S(1)}, s32[1,512]{1,0:T(1,128)S(1)}, s32[1]{0:T(128)}) custom-call(bf16[32,4224]{1,0:T(8,128)(2,1)} %get-tuple-element.86.refs_0_.refs_17_, bf16[32,4224]{1,0:T(8,128)(2,1)} %copy-done.1, bf16[32,4224]{1,0:T(8,128)(2,1)} %copy-done.2, ...), custom_call_target="tpu_custom_call" | custom-call | tf_op jit(solution)/shard_map/collect/pallas_call | solution.py:445
  379.2 11.9 %conditional.1 = (bf16[501,4096]{1,0:T(8,128)(2,1)}) conditional(s32[]{:T(128)} %bitcast.1, (s32[1,1024]{1,0:T(1,128)S(1)}, s32[1,512]{1,0:T(1,128)S(1)}, bf16[256,128,128]{2,1,0:T(8,128)(2,1)}, bf16[512,4096]{1,0:T(8,128)(2,1)}) %tuple.11, (s32[8,1024]{1,0:T(8,128)S(1)}, f32[8,128]{1,0:T(8,128)S(1)}, bf16[1,512,4096]{2,1,0:T(8,128)(2,1)}, ...), branch_computations={%region_0.0_spmd, %region_1.0_spmd} | conditional | bytes 8388616 | solution.py:495
  379.4 11.7 %finish.2 = bf16[501,4096]{1,0:T(8,128)(2,1)} custom-call(s32[1,1024]{1,0:T(1,128)S(1)} %get-tuple-element.34.refs_0_, s32[1,512]{1,0:T(1,128)S(1)} %get-tuple-element.35.refs_1_, bf16[256,128,128]{2,1,0:T(8,128)(2,1)} %get-tuple-element.36.refs_2_, bf16[512,4096]{1,0:T(8,128)(2,1)} %get-tuple-element.37.refs_3_), custom_call_target="tpu_custom_call" | custom-call | tf_op jit(solution)/shard_map/cond/branch_0_fun/finish/pallas_call | solution.py:471
  (88 shorter events, 14.5 us)
Async XLA Ops:
  24.0 355.2 %all-to-all-start.1 = ((bf16[256,128,128]{2,1,0:T(8,128)(2,1)}), bf16[256,128,128]{2,1,0:T(8,128)(2,1)}, u32[]{:S(2)}, u32[]{:S(2)}) async-start(bf16[256,128,128]{2,1,0:T(8,128)(2,1)} %direct.3), calls=%async_computation.1 | async-start | bytes 16777216 | tf_op jit(solution)/shard_map/all_to_all | solution.py:413
  40.6 187.9 %collective-permute-start = (bf16[32,4224]{1,0:T(8,128)(2,1)S(1)}, bf16[32,4224]{1,0:T(8,128)(2,1)S(1)}, u32[]{:S(2)}, u32[]{:S(2)}) collective-permute-start(bf16[32,4224]{1,0:T(8,128)(2,1)S(1)} %copy-done.27), channel_id=1, source_target_pairs={{0,1},{1,2},{2,3},{3,4},{4,5},{5,6},{6,7},{7,0},{8,9},{9,10},{10,1... | collective-permute-start | bytes 811016 | tf_op jit(solution)/shard_map/ppermute | solution.py:391
  42.2 196.5 %collective-permute-start.1 = (bf16[32,4224]{1,0:T(8,128)(2,1)S(1)}, bf16[32,4224]{1,0:T(8,128)(2,1)S(1)}, u32[]{:S(2)}, u32[]{:S(2)}) collective-permute-start(bf16[32,4224]{1,0:T(8,128)(2,1)S(1)} %copy-done.26), channel_id=1, source_target_pairs={{0,2},{1,3},{2,4},{3,5},{4,6},{5,7},{6,0},{7,1},{8,10},{9,11},{10,... | collective-permute-start | bytes 811016 | tf_op jit(solution)/shard_map/ppermute | solution.py:391
  44.8 214.7 %collective-permute-start.2 = (bf16[32,4224]{1,0:T(8,128)(2,1)S(1)}, bf16[32,4224]{1,0:T(8,128)(2,1)S(1)}, u32[]{:S(2)}, u32[]{:S(2)}) collective-permute-start(bf16[32,4224]{1,0:T(8,128)(2,1)S(1)} %copy-done.25), channel_id=1, source_target_pairs={{0,3},{1,4},{2,5},{3,6},{4,7},{5,0},{6,1},{7,2},{8,11},{9,12},{10,... | collective-permute-start | bytes 811016 | tf_op jit(solution)/shard_map/ppermute | solution.py:391
  48.0 222.7 %collective-permute-start.3 = (bf16[32,4224]{1,0:T(8,128)(2,1)S(1)}, bf16[32,4224]{1,0:T(8,128)(2,1)S(1)}, u32[]{:S(2)}, u32[]{:S(2)}) collective-permute-start(bf16[32,4224]{1,0:T(8,128)(2,1)S(1)} %copy-done.24), channel_id=1, source_target_pairs={{0,4},{1,5},{2,6},{3,7},{4,0},{5,1},{6,2},{7,3},{8,12},{9,13},{10,... | collective-permute-start | bytes 811016 | tf_op jit(solution)/shard_map/ppermute | solution.py:391
  49.0 221.7 %collective-permute-start.4 = (bf16[32,4224]{1,0:T(8,128)(2,1)S(1)}, bf16[32,4224]{1,0:T(8,128)(2,1)S(1)}, u32[]{:S(2)}, u32[]{:S(2)}) collective-permute-start(bf16[32,4224]{1,0:T(8,128)(2,1)S(1)} %copy-done.23), channel_id=1, source_target_pairs={{0,5},{1,6},{2,7},{3,0},{4,1},{5,2},{6,3},{7,4},{8,13},{9,14},{10,... | collective-permute-start | bytes 811016 | tf_op jit(solution)/shard_map/ppermute | solution.py:391
  228.5 42.3 %collective-permute-start.5 = (bf16[32,4224]{1,0:T(8,128)(2,1)S(1)}, bf16[32,4224]{1,0:T(8,128)(2,1)S(1)}, u32[]{:S(2)}, u32[]{:S(2)}) collective-permute-start(bf16[32,4224]{1,0:T(8,128)(2,1)S(1)} %copy-done.22), channel_id=1, source_target_pairs={{0,6},{1,7},{2,0},{3,1},{4,2},{5,3},{6,4},{7,5},{8,14},{9,15},{10,... | collective-permute-start | bytes 811016 | tf_op jit(solution)/shard_map/ppermute | solution.py:391
  238.7 32.1 %collective-permute-start.6 = (bf16[32,4224]{1,0:T(8,128)(2,1)S(1)}, bf16[32,4224]{1,0:T(8,128)(2,1)S(1)}, u32[]{:S(2)}, u32[]{:S(2)}) collective-permute-start(bf16[32,4224]{1,0:T(8,128)(2,1)S(1)} %copy-done.21), channel_id=1, source_target_pairs={{0,7},{1,0},{2,1},{3,2},{4,3},{5,4},{6,5},{7,6},{8,15},{9,8},{10,9... | collective-permute-start | bytes 811016 | tf_op jit(solution)/shard_map/ppermute | solution.py:391
  277.8 19.5 %collective-permute-start.7 = (bf16[32,4224]{1,0:T(8,128)(2,1)}, bf16[32,4224]{1,0:T(8,128)(2,1)S(1)}, u32[]{:S(2)}, u32[]{:S(2)}) collective-permute-start(bf16[32,4224]{1,0:T(8,128)(2,1)} %get-tuple-element.87), channel_id=1, source_target_pairs={{0,8},{1,9},{2,10},{3,11},{4,12},{5,13},{6,14},{7,15},{8,16},{9,17... | collective-permute-start | bytes 811016 | tf_op jit(solution)/shard_map/ppermute | solution.py:433
  277.9 19.4 %collective-permute-start.8 = (bf16[32,4224]{1,0:T(8,128)(2,1)}, bf16[32,4224]{1,0:T(8,128)(2,1)S(1)}, u32[]{:S(2)}, u32[]{:S(2)}) collective-permute-start(bf16[32,4224]{1,0:T(8,128)(2,1)} %get-tuple-element.88), channel_id=1, source_target_pairs={{0,16},{1,17},{2,18},{3,19},{4,20},{5,21},{6,22},{7,23},{8,24},{9,... | collective-permute-start | bytes 811016 | tf_op jit(solution)/shard_map/ppermute | solution.py:433
  278.1 19.2 %collective-permute-start.9 = (bf16[32,4224]{1,0:T(8,128)(2,1)}, bf16[32,4224]{1,0:T(8,128)(2,1)S(1)}, u32[]{:S(2)}, u32[]{:S(2)}) collective-permute-start(bf16[32,4224]{1,0:T(8,128)(2,1)} %get-tuple-element.89), channel_id=1, source_target_pairs={{0,24},{1,25},{2,26},{3,27},{4,28},{5,29},{6,30},{7,31},{8,0},{9,1... | collective-permute-start | bytes 811016 | tf_op jit(solution)/shard_map/ppermute | solution.py:433
  280.5 17.0 %collective-permute-start.10 = (bf16[32,4224]{1,0:T(8,128)(2,1)}, bf16[32,4224]{1,0:T(8,128)(2,1)S(1)}, u32[]{:S(2)}, u32[]{:S(2)}) collective-permute-start(bf16[32,4224]{1,0:T(8,128)(2,1)} %get-tuple-element.90), channel_id=1, source_target_pairs={{0,64},{1,65},{2,66},{3,67},{4,68},{5,69},{6,70},{7,71},{8,72},{9,... | collective-permute-start | bytes 811016 | tf_op jit(solution)/shard_map/ppermute | solution.py:433
  280.5 17.1 %collective-permute-start.11 = (bf16[32,4224]{1,0:T(8,128)(2,1)}, bf16[32,4224]{1,0:T(8,128)(2,1)S(1)}, u32[]{:S(2)}, u32[]{:S(2)}) collective-permute-start(bf16[32,4224]{1,0:T(8,128)(2,1)} %get-tuple-element.91), channel_id=1, source_target_pairs={{0,72},{1,73},{2,74},{3,75},{4,76},{5,77},{6,78},{7,79},{8,80},{9,... | collective-permute-start | bytes 811016 | tf_op jit(solution)/shard_map/ppermute | solution.py:433
  297.3 10.2 %collective-permute-start.12 = (bf16[32,4224]{1,0:T(8,128)(2,1)}, bf16[32,4224]{1,0:T(8,128)(2,1)S(1)}, u32[]{:S(2)}, u32[]{:S(2)}) collective-permute-start(bf16[32,4224]{1,0:T(8,128)(2,1)} %get-tuple-element.92), channel_id=1, source_target_pairs={{0,80},{1,81},{2,82},{3,83},{4,84},{5,85},{6,86},{7,87},{8,88},{9,... | collective-permute-start | bytes 811016 | tf_op jit(solution)/shard_map/ppermute | solution.py:433
  297.3 35.6 %collective-permute-start.13 = (bf16[32,4224]{1,0:T(8,128)(2,1)}, bf16[32,4224]{1,0:T(8,128)(2,1)S(1)}, u32[]{:S(2)}, u32[]{:S(2)}) collective-permute-start(bf16[32,4224]{1,0:T(8,128)(2,1)} %get-tuple-element.93), channel_id=1, source_target_pairs={{0,88},{1,89},{2,90},{3,91},{4,92},{5,93},{6,94},{7,95},{8,64},{9,... | collective-permute-start | bytes 811016 | tf_op jit(solution)/shard_map/ppermute | solution.py:433
  297.4 35.5 %collective-permute-start.14 = (bf16[32,4224]{1,0:T(8,128)(2,1)}, bf16[32,4224]{1,0:T(8,128)(2,1)S(1)}, u32[]{:S(2)}, u32[]{:S(2)}) collective-permute-start(bf16[32,4224]{1,0:T(8,128)(2,1)} %get-tuple-element.94), channel_id=1, source_target_pairs={{0,128},{1,129},{2,130},{3,131},{4,132},{5,133},{6,134},{7,135},{8... | collective-permute-start | bytes 811016 | tf_op jit(solution)/shard_map/ppermute | solution.py:433
  297.5 35.5 %collective-permute-start.15 = (bf16[32,4224]{1,0:T(8,128)(2,1)}, bf16[32,4224]{1,0:T(8,128)(2,1)S(1)}, u32[]{:S(2)}, u32[]{:S(2)}) collective-permute-start(bf16[32,4224]{1,0:T(8,128)(2,1)} %get-tuple-element.95), channel_id=1, source_target_pairs={{0,136},{1,137},{2,138},{3,139},{4,140},{5,141},{6,142},{7,143},{8... | collective-permute-start | bytes 811016 | tf_op jit(solution)/shard_map/ppermute | solution.py:433
  297.6 39.0 %collective-permute-start.16 = (bf16[32,4224]{1,0:T(8,128)(2,1)}, bf16[32,4224]{1,0:T(8,128)(2,1)S(1)}, u32[]{:S(2)}, u32[]{:S(2)}) collective-permute-start(bf16[32,4224]{1,0:T(8,128)(2,1)} %get-tuple-element.96), channel_id=1, source_target_pairs={{0,144},{1,145},{2,146},{3,147},{4,148},{5,149},{6,150},{7,151},{8... | collective-permute-start | bytes 811016 | tf_op jit(solution)/shard_map/ppermute | solution.py:433
  307.4 29.2 %collective-permute-start.17 = (bf16[32,4224]{1,0:T(8,128)(2,1)}, bf16[32,4224]{1,0:T(8,128)(2,1)S(1)}, u32[]{:S(2)}, u32[]{:S(2)}) collective-permute-start(bf16[32,4224]{1,0:T(8,128)(2,1)} %get-tuple-element.97), channel_id=1, source_target_pairs={{0,152},{1,153},{2,154},{3,155},{4,156},{5,157},{6,158},{7,159},{8... | collective-permute-start | bytes 811016 | tf_op jit(solution)/shard_map/ppermute | solution.py:433
  332.9 5.5 %collective-permute-start.18 = (bf16[32,4224]{1,0:T(8,128)(2,1)}, bf16[32,4224]{1,0:T(8,128)(2,1)S(1)}, u32[]{:S(2)}, u32[]{:S(2)}) collective-permute-start(bf16[32,4224]{1,0:T(8,128)(2,1)} %get-tuple-element.98), channel_id=1, source_target_pairs={{0,192},{1,193},{2,194},{3,195},{4,196},{5,197},{6,198},{7,199},{8... | collective-permute-start | bytes 811016 | tf_op jit(solution)/shard_map/ppermute | solution.py:433
  332.9 11.7 %collective-permute-start.19 = (bf16[32,4224]{1,0:T(8,128)(2,1)}, bf16[32,4224]{1,0:T(8,128)(2,1)S(1)}, u32[]{:S(2)}, u32[]{:S(2)}) collective-permute-start(bf16[32,4224]{1,0:T(8,128)(2,1)} %get-tuple-element.99), channel_id=1, source_target_pairs={{0,200},{1,201},{2,202},{3,203},{4,204},{5,205},{6,206},{7,207},{8... | collective-permute-start | bytes 811016 | tf_op jit(solution)/shard_map/ppermute | solution.py:433
  333.0 15.4 %collective-permute-start.20 = (bf16[32,4224]{1,0:T(8,128)(2,1)}, bf16[32,4224]{1,0:T(8,128)(2,1)}, u32[]{:S(2)}, u32[]{:S(2)}) collective-permute-start(bf16[32,4224]{1,0:T(8,128)(2,1)} %get-tuple-element.100), channel_id=1, source_target_pairs={{0,208},{1,209},{2,210},{3,211},{4,212},{5,213},{6,214},{7,215},{8... | collective-permute-start | bytes 811016 | tf_op jit(solution)/shard_map/ppermute | solution.py:433
  336.6 22.7 %collective-permute-start.21 = (bf16[32,4224]{1,0:T(8,128)(2,1)}, bf16[32,4224]{1,0:T(8,128)(2,1)}, u32[]{:S(2)}, u32[]{:S(2)}) collective-permute-start(bf16[32,4224]{1,0:T(8,128)(2,1)} %get-tuple-element.101), channel_id=1, source_target_pairs={{0,216},{1,217},{2,218},{3,219},{4,220},{5,221},{6,222},{7,223},{8... | collective-permute-start | bytes 811016 | tf_op jit(solution)/shard_map/ppermute | solution.py:433
  363.6 8.0 %collective-permute-start.22 = (bf16[256,4224]{1,0:T(8,128)(2,1)}, bf16[256,4224]{1,0:T(8,128)(2,1)S(1)}, u32[]{:S(2)}, u32[]{:S(2)}) collective-permute-start(bf16[256,4224]{1,0:T(8,128)(2,1)} %stack.1), channel_id=1, source_target_pairs={{0,32},{1,33},{2,34},{3,35},{4,36},{5,37},{6,38},{7,39},{8,40},{9,... | collective-permute-start | bytes 6488072 | tf_op jit(solution)/shard_map/ppermute | solution.py:443
  (28 other events, 1137.6 us)

commit v3 on v2

--- a/solution.py
+++ b/solution.py
@@ -112,7 +112,7 @@
     rows[half:] = (weight[0:1, 0:1] * rg[0].astype(f32)).astype(bf16)
 
 
-def first_kernel(cid, rid, lengths, clogp, rlogp, ref, cg, rg, *refs, row_count):
+def first_kernel(cid, rid, clen, rlen, clogp, rlogp, ref, cg, rg, *refs, row_count):
     outs = refs[:ZS]
     plan, weight, note, pick, rows, arrival = refs[ZS:]
     step = pl.program_id(0)
@@ -136,7 +136,7 @@
                 fetch.start()
         route(cid, rid, plan, note, row_count)
         weight[...] = jnp.broadcast_to(
-            pair_weight(lengths[0], lengths[1], clogp, rlogp, ref), weight.shape
+            pair_weight(clen[0], rlen[0], clogp, rlogp, ref), weight.shape
         )
         pick[...] = onehot(iota(pick.shape, 0) == plan[1:2])
 
@@ -229,14 +229,19 @@
     place = here()
     parts = refs[: TURNS + 1]
     notes = refs[TURNS + 1 : 2 * TURNS + 2]
-    rows, near, far, late, flag = refs[2 * TURNS + 2 :]
+    *rows, near, far, late, flag = refs[2 * TURNS + 2 :]
     each = ZS * REST
     count = PLANE * each
     owners = PLANE * ZS
-    start = 0
-    for part in parts:
-        rows[start : start + part.shape[0]] = part[...]
-        start += part.shape[0]
+    last = pl.num_programs(0) - 1
+    for out, now in zip(rows, (pl.program_id(0) < last, pl.program_id(0) == last)):
+
+        @pl.when(now)
+        def _():
+            start = 0
+            for part in parts:
+                out[start : start + part.shape[0]] = part[...]
+                start += part.shape[0]
 
     @pl.when(pl.program_id(0) == 0)
     def _():
@@ -280,17 +285,19 @@
 def finish_kernel(*refs, tiled):
     labels = refs[: tiled + 1]
     packed = refs[tiled + 1 : 2 * tiled + 1]
-    rest = refs[2 * tiled + 1]
-    out, pick, *scratch = refs[2 * tiled + 2 : 2 * tiled + 8]
-    *blocks, others, arrival = refs[2 * tiled + 8 :]
+    rest = refs[2 * tiled + 1 : 2 * tiled + 3]
+    out, pick, *scratch = refs[2 * tiled + 3 : 2 * tiled + 9]
+    *blocks, others, arrival = refs[2 * tiled + 9 :]
     step = pl.program_id(0)
-
-    def fetches(n):
+    split = rest[0].shape[1] // STEP
+
+    def fetches(n, late):
         pairs = []
         for source, block in zip(packed, blocks):
             tall = block.shape[2]
             pairs.append((source.at[:, pl.ds(n * tall, tall)], block.at[n]))
-        pairs.append((rest.at[:, pl.ds(n * STEP, STEP)], others.at[n]))
+        column = (n - split * late) * STEP
+        pairs.append((rest[late].at[:, pl.ds(column, STEP)], others.at[n]))
         return [
             pltpu.make_async_copy(source, target, arrival.at[n, i])
             for i, (source, target) in enumerate(pairs)
@@ -299,7 +306,7 @@
     @pl.when(step == 0)
     def _():
         for n in range(others.shape[0]):
-            for fetch in fetches(n):
+            for fetch in fetches(n, int(n >= split)):
                 fetch.start()
         start = 0
         for label in labels:
@@ -308,9 +315,14 @@
             part[...] = onehot(iota(part.shape, 0) == label[...])
             start += size
 
-    for fetch in fetches(step):
-        fetch.wait()
-    total = dot(pick[:, -rest.shape[0] :], others[step])
+    for late in range(2):
+
+        @pl.when((step >= split) == bool(late))
+        def _():
+            for fetch in fetches(step, late):
+                fetch.wait()
+
+    total = dot(pick[:, -others.shape[1] :], others[step])
     start = 0
     for block in blocks:
         _, count, tall, width = block.shape
@@ -364,7 +376,7 @@
         + [jax.ShapeDtypeStruct((8, tokens), i32), jax.ShapeDtypeStruct((8, 128), f32)],
         grid=(few + 1,),
         in_specs=[whole(1, length)] * 2
-        + [smem]
+        + [smem] * 2
         + [whole(1, length)] * 2
         + [smem] + [pl.BlockSpec(memory_space=pl.ANY)] * 2,
         out_specs=[pl.BlockSpec((LIMIT, WIDE), lambda n: (0, n))] * ZS
@@ -379,7 +391,8 @@
     )(
         cid,
         rid,
-        jnp.concatenate([clen, rlen]),
+        clen,
+        rlen,
         clogp,
         rlogp,
         ref.reshape(2),
@@ -442,10 +455,11 @@
     )(*turns)
     swap = lax.ppermute(swap, axes, shifted(0, 1, 0, 0))
 
-    rest, near, far, late, flag = pl.pallas_call(
+    *rest, near, far, late, flag = pl.pallas_call(
         collect_kernel,
         out_shape=[
-            jax.ShapeDtypeStruct((PLANE * each, features), bf16),
+            jax.ShapeDtypeStruct((PLANE * each, features - WIDE), bf16),
+            jax.ShapeDtypeStruct((PLANE * each, WIDE), bf16),
             jax.ShapeDtypeStruct((1, owners * DIRECT), i32),
             jax.ShapeDtypeStruct((1, PLANE * each), i32),
             jax.ShapeDtypeStruct((1, owners * REST), i32),
@@ -457,7 +471,8 @@
         + [pl.BlockSpec((each, NOTE), lambda n: (0, features // NOTE))] * TURNS
         + [pl.BlockSpec((TURNS * each, NOTE), lambda n: (0, features // NOTE))],
         out_specs=[
-            pl.BlockSpec((PLANE * each, WIDE), lambda n: (0, n)),
+            pl.BlockSpec((PLANE * each, WIDE), lambda n: (0, jnp.minimum(n, few - 2))),
+            whole(PLANE * each, WIDE),
             whole(1, owners * DIRECT),
             whole(1, PLANE * each),
             whole(1, owners * REST),
@@ -473,7 +488,7 @@
             out_shape=jax.ShapeDtypeStruct((row_count, features), bf16),
             grid=(steps,),
             in_specs=[whole(*label.shape) for label in labels]
-            + [pl.BlockSpec(memory_space=pl.ANY)] * (len(packed) + 1),
+            + [pl.BlockSpec(memory_space=pl.ANY)] * (len(packed) + 2),
             out_specs=pl.BlockSpec((row_count, STEP), lambda n: (0, n)),
             scratch_shapes=[pltpu.VMEM((padded, count), bf16)]
             + [
@@ -490,7 +505,7 @@
                 pltpu.SemaphoreType.DMA((steps, len(packed) + 1)),
             ],
             name="finish",
-        )(*labels, *packed, rest)
+        )(*labels, *packed, *rest)
 
     return lax.cond(
         flag[0] > 0,

time: 392 us -> 390 us (level)
  no operation moved by 1% of the time
where the time goes in v3:
time: 390 us; the launch traced here: 389 us
  waiting for transfers between devices  283 us (73%)
  starting transfers between devices  53.2 us (14%)
  Pallas kernels  48.9 us (13%)
    ppermute x7, waiting for transfers between devices, local(): hopped[d] = lax.ppermute(first[d], axes, shifted(0, 0, 0, d))  214 us
    ppermute x15, waiting for transfers between devices, local(): lax.ppermute(second[e], axes, shifted(e // YS, 0, e % YS, 0))  64.9 us
    all_to_all x1, starting transfers between devices, direct(): return lax.all_to_all(sent, axes, split_axis=0, concat_axis=0, tiled=True)  16.7 us
    ppermute x15, starting transfers between devices, local(): lax.ppermute(second[e], axes, shifted(e // YS, 0, e % YS, 0))  16.5 us
    ppermute x7, starting transfers between devices, local(): hopped[d] = lax.ppermute(first[d], axes, shifted(0, 0, 0, d))  16.2 us
    pallas_call x1, Pallas kernels, direct(): pl.pallas_call(functools.partial(direct_kernel, kind=kind), out_shape=jax...  14.5 us
    pallas_call x1, Pallas kernels, finish(): pl.pallas_call(functools.partial(finish_kernel, tiled=len(packed)), out_s...  11.5 us
  transfers between devices with their start and end apart: 24, of which 11 were waited for; matrix products, arithmetic and copies ran while one was open for 0% of the time, Pallas kernels for 4%

profile of v3, /device:TPU:1, one launch (start us, length us, event | category | flops | bytes accessed | tf_op | source)
XLA Modules:
  0.0 389.0 jit_solution(17722242748621035473)
XLA Ops:
  1.3 7.5 %first.1 = (bf16[32,4224]{1,0:T(8,128)(2,1)}, bf16[32,4224]{1,0:T(8,128)(2,1)}, bf16[32,4224]{1,0:T(8,128)(2,1)}, bf16[32,4224]{1,0:T(8,128)(2,1)}, bf16[32,4224...) custom-call(s32[1,512]{1,0:T(1,128)} %cid.1, ...), custom_call_target="tpu_custom_call" | custom-call | tf_op jit(solution)/shard_map/first/pallas_call | solution.py:373
  8.8 14.5 %direct.3 = bf16[256,128,128]{2,1,0:T(8,128)(2,1)} custom-call(s32[8,1024]{1,0:T(8,128)S(1)} %get-tuple-element.112.plan, f32[8,128]{1,0:T(8,128)S(1)} %get-tuple-element.113.weight, bf16[1,512,4096]{2,1,0:T(8,128)(2,1)} %cg.3, bf16[1,512,4096]{2,1,0:T(8,128)(2,1)} %rg.3), custom_call_target="tpu_custom_call" | custom-call | tf_op jit(solution)/shard_map/direct/pallas_call | solution.py:408
  23.4 16.7 %all-to-all-start.1 = ((bf16[256,128,128]{2,1,0:T(8,128)(2,1)}), bf16[256,128,128]{2,1,0:T(8,128)(2,1)}, u32[]{:S(2)}, u32[]{:S(2)}) async-start(bf16[256,128,128]{2,1,0:T(8,128)(2,1)} %direct.3), calls=%async_computation.1 | async-start | bytes 16777216 | tf_op jit(solution)/shard_map/all_to_all | solution.py:426
  41.6 2.6 collective-permute-start.1
  44.2 3.2 collective-permute-start.2
  48.4 3.7 collective-permute-start.4
  52.2 175.7 %collective-permute-done.refs_1_.refs_9_ = bf16[32,4224]{1,0:T(8,128)(2,1)S(1)} collective-permute-done((bf16[32,4224]{1,0:T(8,128)(2,1)S(1)}, bf16[32,4224]{1,0:T(8,128)(2,1)S(1)}, u32[]{:S(2)}, u32[]{:S(2)}) %collective-permute-start) | collective-permute-done | bytes 270368 | tf_op jit(solution)/shard_map/ppermute | solution.py:404
  229.7 8.4 %collective-permute-done.1.refs_2_.refs_10_ = bf16[32,4224]{1,0:T(8,128)(2,1)S(1)} collective-permute-done((bf16[32,4224]{1,0:T(8,128)(2,1)S(1)}, bf16[32,4224]{1,0:T(8,128)(2,1)S(1)}, u32[]{:S(2)}, u32[]{:S(2)}) %collective-permute-start.1) | collective-permute-done | bytes 270368 | tf_op jit(solution)/shard_map/ppermute | solution.py:404
  240.4 18.6 %collective-permute-done.2.refs_3_.refs_11_ = bf16[32,4224]{1,0:T(8,128)(2,1)S(1)} collective-permute-done((bf16[32,4224]{1,0:T(8,128)(2,1)S(1)}, bf16[32,4224]{1,0:T(8,128)(2,1)S(1)}, u32[]{:S(2)}, u32[]{:S(2)}) %collective-permute-start.2) | collective-permute-done | bytes 270368 | tf_op jit(solution)/shard_map/ppermute | solution.py:404
  258.9 11.2 %collective-permute-done.3.refs_4_.refs_12_ = bf16[32,4224]{1,0:T(8,128)(2,1)S(1)} collective-permute-done((bf16[32,4224]{1,0:T(8,128)(2,1)S(1)}, bf16[32,4224]{1,0:T(8,128)(2,1)S(1)}, u32[]{:S(2)}, u32[]{:S(2)}) %collective-permute-start.3) | collective-permute-done | bytes 270368 | tf_op jit(solution)/shard_map/ppermute | solution.py:404
  271.2 6.0 %second.1 = (bf16[32,4224]{1,0:T(8,128)(2,1)}, bf16[32,4224]{1,0:T(8,128)(2,1)}, bf16[32,4224]{1,0:T(8,128)(2,1)}, bf16[32,4224]{1,0:T(8,128)(2,1)}, bf16[32,422...) custom-call(bf16[32,4224]{1,0:T(8,128)(2,1)} %get-tuple-element.85.r, ...), custom_call_target="tpu_custom_call" | custom-call | tf_op jit(solution)/shard_map/second/pallas_call | solution.py:433
  280.0 16.7 %collective-permute-done.7.refs_1_.refs_18_ = bf16[32,4224]{1,0:T(8,128)(2,1)S(1)} collective-permute-done((bf16[32,4224]{1,0:T(8,128)(2,1)}, bf16[32,4224]{1,0:T(8,128)(2,1)S(1)}, u32[]{:S(2)}, u32[]{:S(2)}) %collective-permute-start.7) | collective-permute-done | bytes 270368 | tf_op jit(solution)/shard_map/ppermute | solution.py:446
  297.1 9.8 %collective-permute-start.16 = (bf16[32,4224]{1,0:T(8,128)(2,1)}, bf16[32,4224]{1,0:T(8,128)(2,1)S(1)}, u32[]{:S(2)}, u32[]{:S(2)}) collective-permute-start(bf16[32,4224]{1,0:T(8,128)(2,1)} %get-tuple-element.103), channel_id=1, source_target_pairs={{0,144},{1,145},{2,146},{3,147},{4,148},{5,149},{6,150},{7,151},{8... | collective-permute-start | bytes 811016 | tf_op jit(solution)/shard_map/ppermute | solution.py:446
  306.9 25.5 %collective-permute-done.13.refs_7_.refs_24_ = bf16[32,4224]{1,0:T(8,128)(2,1)S(1)} collective-permute-done((bf16[32,4224]{1,0:T(8,128)(2,1)}, bf16[32,4224]{1,0:T(8,128)(2,1)S(1)}, u32[]{:S(2)}, u32[]{:S(2)}) %collective-permute-start.13) | collective-permute-done | bytes 270368 | tf_op jit(solution)/shard_map/ppermute | solution.py:446
  332.5 3.6 collective-permute-start.20
  337.9 6.3 %collective-permute-done.19.refs_13_.refs_30_ = bf16[32,4224]{1,0:T(8,128)(2,1)} collective-permute-done((bf16[32,4224]{1,0:T(8,128)(2,1)}, bf16[32,4224]{1,0:T(8,128)(2,1)}, u32[]{:S(2)}, u32[]{:S(2)}) %collective-permute-start.19) | collective-permute-done | bytes 270368 | tf_op jit(solution)/shard_map/ppermute | solution.py:446
  344.2 3.6 collective-permute-done.20.refs_14_.refs_31_
  347.8 11.0 %collective-permute-done.21.refs_15_.refs_32_ = bf16[32,4224]{1,0:T(8,128)(2,1)} collective-permute-done((bf16[32,4224]{1,0:T(8,128)(2,1)}, bf16[32,4224]{1,0:T(8,128)(2,1)}, u32[]{:S(2)}, u32[]{:S(2)}) %collective-permute-start.21) | collective-permute-done | bytes 270368 | tf_op jit(solution)/shard_map/ppermute | solution.py:446
  358.9 4.1 %stack.1 = bf16[256,4224]{1,0:T(8,128)(2,1)} custom-call(bf16[32,4224]{1,0:T(8,128)(2,1)} %get-tuple-element.93.refs_0_.refs_17_, bf16[32,4224]{1,0:T(8,128)(2,1)} %copy-done, bf16[32,4224]{1,0:T(8,128)(2,1)} %copy-done.1, bf16[32,4224]{1,0:T(8,128)(2,1)} %copy-done.2, bf16[32,4224]{1,0:T(8,128)(2,1)} %copy-done.3, bf16[32,4224]{1,0:T(8,128)(2,1)} %copy-done.4, ...), custom_call_target="tpu_custom_call" | custom-call | tf_op jit(solution)/shard_map/stack/pallas_call | solution.py:448
  363.0 3.9 %collective-permute-start.22 = (bf16[256,4224]{1,0:T(8,128)(2,1)}, bf16[256,4224]{1,0:T(8,128)(2,1)}, u32[]{:S(2)}, u32[]{:S(2)}) collective-permute-start(bf16[256,4224]{1,0:T(8,128)(2,1)} %stack.1), channel_id=1, source_target_pairs={{0,32},{1,33},{2,34},{3,35},{4,36},{5,37},{6,38},{7,39},{8,40},{9,... | collective-permute-start | bytes 6488072 | tf_op jit(solution)/shard_map/ppermute | solution.py:456
  366.9 4.2 %collective-permute-done.22.refs_16_.refs_33_ = bf16[256,4224]{1,0:T(8,128)(2,1)} collective-permute-done((bf16[256,4224]{1,0:T(8,128)(2,1)}, bf16[256,4224]{1,0:T(8,128)(2,1)}, u32[]{:S(2)}, u32[]{:S(2)}) %collective-permute-start.22) | collective-permute-done | bytes 2162720 | tf_op jit(solution)/shard_map/ppermute | solution.py:456
  371.2 5.2 %collect.1 = (bf16[512,3072]{1,0:T(8,128)(2,1)S(1)}, bf16[512,1024]{1,0:T(8,128)(2,1)}, s32[1,1024]{1,0:T(1,128)S(1)}, s32[1,512]{1,0:T(1,128)S(1)}, s32[1,512]{1,0:T(1,128)S(1)}, /*index=5*/s32[1]{0:T(128)}) custom-call(bf16[32,4224]{1,0:T(8,128)(2,1)} %get-tuple-element.93.refs_0_.refs_17_, bf16[32,4224]{1,0:T(8,128)(2,1)} %copy-done, ...), custom_call_target="tpu_custom_call" | custom-call | tf_op jit(solution)/shard_map/collect/pallas_call | solution.py:458
  377.0 11.8 %conditional.1 = (bf16[501,4096]{1,0:T(8,128)(2,1)}) conditional(s32[]{:T(128)} %bitcast.1, (s32[1,1024]{1,0:T(1,128)S(1)}, s32[1,512]{1,0:T(1,128)S(1)}, bf16[256,128,128]{2,1,0:T(8,128)(2,1)}, bf16[512,3072]{1,0:T(8,128)(2,1)S(1)}, bf16[512,1024]{1,0:T(8,128)(2,1)}) %tuple.11, (s32[8,1024]{1,0:T(8,128)S(1)}, f32[8,128]{1,0:T(8,128)S(1)}, ...), branch_computations={%region_0.0_spmd, %region_1.0_spmd} | conditional | bytes 8388616 | solution.py:510
  377.3 11.5 %finish.2 = bf16[501,4096]{1,0:T(8,128)(2,1)} custom-call(s32[1,1024]{1,0:T(1,128)S(1)} %get-tuple-element.38.refs_0_, s32[1,512]{1,0:T(1,128)S(1)} %get-tuple-element.39.refs_1_, bf16[256,128,128]{2,1,0:T(8,128)(2,1)} %get-tuple-element.40.refs_2_, bf16[512,3072]{1,0:T(8,128)(2,1)S(1)} %get-tuple-element.41.refs_3_, bf16[512,1024]{1,0:T(8,128)(2,1)} %get-tuple-element.42.refs_4_), custom_call_target="tpu_custom_call" | custom-call | tf_op jit(solution)/shard_map/cond/branch_0_fun/finish/pallas_call | solution.py:486
  (83 shorter events, 12.6 us)
Async XLA Ops:
  23.4 353.7 %all-to-all-start.1 = ((bf16[256,128,128]{2,1,0:T(8,128)(2,1)}), bf16[256,128,128]{2,1,0:T(8,128)(2,1)}, u32[]{:S(2)}, u32[]{:S(2)}) async-start(bf16[256,128,128]{2,1,0:T(8,128)(2,1)} %direct.3), calls=%async_computation.1 | async-start | bytes 16777216 | tf_op jit(solution)/shard_map/all_to_all | solution.py:426
  40.0 187.9 %collective-permute-start = (bf16[32,4224]{1,0:T(8,128)(2,1)S(1)}, bf16[32,4224]{1,0:T(8,128)(2,1)S(1)}, u32[]{:S(2)}, u32[]{:S(2)}) collective-permute-start(bf16[32,4224]{1,0:T(8,128)(2,1)S(1)} %copy-done.25), channel_id=1, source_target_pairs={{0,1},{1,2},{2,3},{3,4},{4,5},{5,6},{6,7},{7,0},{8,9},{9,10},{10,1... | collective-permute-start | bytes 811016 | tf_op jit(solution)/shard_map/ppermute | solution.py:404
  41.6 196.5 %collective-permute-start.1 = (bf16[32,4224]{1,0:T(8,128)(2,1)S(1)}, bf16[32,4224]{1,0:T(8,128)(2,1)S(1)}, u32[]{:S(2)}, u32[]{:S(2)}) collective-permute-start(bf16[32,4224]{1,0:T(8,128)(2,1)S(1)} %copy-done.24), channel_id=1, source_target_pairs={{0,2},{1,3},{2,4},{3,5},{4,6},{5,7},{6,0},{7,1},{8,10},{9,11},{10,... | collective-permute-start | bytes 811016 | tf_op jit(solution)/shard_map/ppermute | solution.py:404
  44.2 214.7 %collective-permute-start.2 = (bf16[32,4224]{1,0:T(8,128)(2,1)S(1)}, bf16[32,4224]{1,0:T(8,128)(2,1)S(1)}, u32[]{:S(2)}, u32[]{:S(2)}) collective-permute-start(bf16[32,4224]{1,0:T(8,128)(2,1)S(1)} %copy-done.23), channel_id=1, source_target_pairs={{0,3},{1,4},{2,5},{3,6},{4,7},{5,0},{6,1},{7,2},{8,11},{9,12},{10,... | collective-permute-start | bytes 811016 | tf_op jit(solution)/shard_map/ppermute | solution.py:404
  47.4 222.7 %collective-permute-start.3 = (bf16[32,4224]{1,0:T(8,128)(2,1)S(1)}, bf16[32,4224]{1,0:T(8,128)(2,1)S(1)}, u32[]{:S(2)}, u32[]{:S(2)}) collective-permute-start(bf16[32,4224]{1,0:T(8,128)(2,1)S(1)} %copy-done.22), channel_id=1, source_target_pairs={{0,4},{1,5},{2,6},{3,7},{4,0},{5,1},{6,2},{7,3},{8,12},{9,13},{10,... | collective-permute-start | bytes 811016 | tf_op jit(solution)/shard_map/ppermute | solution.py:404
  48.4 221.7 %collective-permute-start.4 = (bf16[32,4224]{1,0:T(8,128)(2,1)S(1)}, bf16[32,4224]{1,0:T(8,128)(2,1)S(1)}, u32[]{:S(2)}, u32[]{:S(2)}) collective-permute-start(bf16[32,4224]{1,0:T(8,128)(2,1)S(1)} %copy-done.21), channel_id=1, source_target_pairs={{0,5},{1,6},{2,7},{3,0},{4,1},{5,2},{6,3},{7,4},{8,13},{9,14},{10,... | collective-permute-start | bytes 811016 | tf_op jit(solution)/shard_map/ppermute | solution.py:404
  227.9 42.3 %collective-permute-start.5 = (bf16[32,4224]{1,0:T(8,128)(2,1)S(1)}, bf16[32,4224]{1,0:T(8,128)(2,1)S(1)}, u32[]{:S(2)}, u32[]{:S(2)}) collective-permute-start(bf16[32,4224]{1,0:T(8,128)(2,1)S(1)} %copy-done.20), channel_id=1, source_target_pairs={{0,6},{1,7},{2,0},{3,1},{4,2},{5,3},{6,4},{7,5},{8,14},{9,15},{10,... | collective-permute-start | bytes 811016 | tf_op jit(solution)/shard_map/ppermute | solution.py:404
  238.1 32.1 %collective-permute-start.6 = (bf16[32,4224]{1,0:T(8,128)(2,1)S(1)}, bf16[32,4224]{1,0:T(8,128)(2,1)S(1)}, u32[]{:S(2)}, u32[]{:S(2)}) collective-permute-start(bf16[32,4224]{1,0:T(8,128)(2,1)S(1)} %copy-done.19), channel_id=1, source_target_pairs={{0,7},{1,0},{2,1},{3,2},{4,3},{5,4},{6,5},{7,6},{8,15},{9,8},{10,9... | collective-permute-start | bytes 811016 | tf_op jit(solution)/shard_map/ppermute | solution.py:404
  277.2 19.5 %collective-permute-start.7 = (bf16[32,4224]{1,0:T(8,128)(2,1)}, bf16[32,4224]{1,0:T(8,128)(2,1)S(1)}, u32[]{:S(2)}, u32[]{:S(2)}) collective-permute-start(bf16[32,4224]{1,0:T(8,128)(2,1)} %get-tuple-element.94), channel_id=1, source_target_pairs={{0,8},{1,9},{2,10},{3,11},{4,12},{5,13},{6,14},{7,15},{8,16},{9,17... | collective-permute-start | bytes 811016 | tf_op jit(solution)/shard_map/ppermute | solution.py:446
  277.3 19.4 %collective-permute-start.8 = (bf16[32,4224]{1,0:T(8,128)(2,1)}, bf16[32,4224]{1,0:T(8,128)(2,1)S(1)}, u32[]{:S(2)}, u32[]{:S(2)}) collective-permute-start(bf16[32,4224]{1,0:T(8,128)(2,1)} %get-tuple-element.95), channel_id=1, source_target_pairs={{0,16},{1,17},{2,18},{3,19},{4,20},{5,21},{6,22},{7,23},{8,24},{9,... | collective-permute-start | bytes 811016 | tf_op jit(solution)/shard_map/ppermute | solution.py:446
  277.6 19.2 %collective-permute-start.9 = (bf16[32,4224]{1,0:T(8,128)(2,1)}, bf16[32,4224]{1,0:T(8,128)(2,1)S(1)}, u32[]{:S(2)}, u32[]{:S(2)}) collective-permute-start(bf16[32,4224]{1,0:T(8,128)(2,1)} %get-tuple-element.96), channel_id=1, source_target_pairs={{0,24},{1,25},{2,26},{3,27},{4,28},{5,29},{6,30},{7,31},{8,0},{9,1... | collective-permute-start | bytes 811016 | tf_op jit(solution)/shard_map/ppermute | solution.py:446
  279.9 17.0 %collective-permute-start.10 = (bf16[32,4224]{1,0:T(8,128)(2,1)}, bf16[32,4224]{1,0:T(8,128)(2,1)S(1)}, u32[]{:S(2)}, u32[]{:S(2)}) collective-permute-start(bf16[32,4224]{1,0:T(8,128)(2,1)} %get-tuple-element.97), channel_id=1, source_target_pairs={{0,64},{1,65},{2,66},{3,67},{4,68},{5,69},{6,70},{7,71},{8,72},{9,... | collective-permute-start | bytes 811016 | tf_op jit(solution)/shard_map/ppermute | solution.py:446
  280.0 17.1 %collective-permute-start.11 = (bf16[32,4224]{1,0:T(8,128)(2,1)}, bf16[32,4224]{1,0:T(8,128)(2,1)S(1)}, u32[]{:S(2)}, u32[]{:S(2)}) collective-permute-start(bf16[32,4224]{1,0:T(8,128)(2,1)} %get-tuple-element.98), channel_id=1, source_target_pairs={{0,72},{1,73},{2,74},{3,75},{4,76},{5,77},{6,78},{7,79},{8,80},{9,... | collective-permute-start | bytes 811016 | tf_op jit(solution)/shard_map/ppermute | solution.py:446
  296.7 10.2 %collective-permute-start.12 = (bf16[32,4224]{1,0:T(8,128)(2,1)}, bf16[32,4224]{1,0:T(8,128)(2,1)S(1)}, u32[]{:S(2)}, u32[]{:S(2)}) collective-permute-start(bf16[32,4224]{1,0:T(8,128)(2,1)} %get-tuple-element.99), channel_id=1, source_target_pairs={{0,80},{1,81},{2,82},{3,83},{4,84},{5,85},{6,86},{7,87},{8,88},{9,... | collective-permute-start | bytes 811016 | tf_op jit(solution)/shard_map/ppermute | solution.py:446
  296.7 35.6 %collective-permute-start.13 = (bf16[32,4224]{1,0:T(8,128)(2,1)}, bf16[32,4224]{1,0:T(8,128)(2,1)S(1)}, u32[]{:S(2)}, u32[]{:S(2)}) collective-permute-start(bf16[32,4224]{1,0:T(8,128)(2,1)} %get-tuple-element.100), channel_id=1, source_target_pairs={{0,88},{1,89},{2,90},{3,91},{4,92},{5,93},{6,94},{7,95},{8,64},{9,... | collective-permute-start | bytes 811016 | tf_op jit(solution)/shard_map/ppermute | solution.py:446
  296.8 35.5 %collective-permute-start.14 = (bf16[32,4224]{1,0:T(8,128)(2,1)}, bf16[32,4224]{1,0:T(8,128)(2,1)S(1)}, u32[]{:S(2)}, u32[]{:S(2)}) collective-permute-start(bf16[32,4224]{1,0:T(8,128)(2,1)} %get-tuple-element.101), channel_id=1, source_target_pairs={{0,128},{1,129},{2,130},{3,131},{4,132},{5,133},{6,134},{7,135},{8... | collective-permute-start | bytes 811016 | tf_op jit(solution)/shard_map/ppermute | solution.py:446
  296.9 35.5 %collective-permute-start.15 = (bf16[32,4224]{1,0:T(8,128)(2,1)}, bf16[32,4224]{1,0:T(8,128)(2,1)S(1)}, u32[]{:S(2)}, u32[]{:S(2)}) collective-permute-start(bf16[32,4224]{1,0:T(8,128)(2,1)} %get-tuple-element.102), channel_id=1, source_target_pairs={{0,136},{1,137},{2,138},{3,139},{4,140},{5,141},{6,142},{7,143},{8... | collective-permute-start | bytes 811016 | tf_op jit(solution)/shard_map/ppermute | solution.py:446
  297.1 39.0 %collective-permute-start.16 = (bf16[32,4224]{1,0:T(8,128)(2,1)}, bf16[32,4224]{1,0:T(8,128)(2,1)S(1)}, u32[]{:S(2)}, u32[]{:S(2)}) collective-permute-start(bf16[32,4224]{1,0:T(8,128)(2,1)} %get-tuple-element.103), channel_id=1, source_target_pairs={{0,144},{1,145},{2,146},{3,147},{4,148},{5,149},{6,150},{7,151},{8... | collective-permute-start | bytes 811016 | tf_op jit(solution)/shard_map/ppermute | solution.py:446
  306.9 29.2 %collective-permute-start.17 = (bf16[32,4224]{1,0:T(8,128)(2,1)}, bf16[32,4224]{1,0:T(8,128)(2,1)S(1)}, u32[]{:S(2)}, u32[]{:S(2)}) collective-permute-start(bf16[32,4224]{1,0:T(8,128)(2,1)} %get-tuple-element.104), channel_id=1, source_target_pairs={{0,152},{1,153},{2,154},{3,155},{4,156},{5,157},{6,158},{7,159},{8... | collective-permute-start | bytes 811016 | tf_op jit(solution)/shard_map/ppermute | solution.py:446
  332.3 5.5 %collective-permute-start.18 = (bf16[32,4224]{1,0:T(8,128)(2,1)}, bf16[32,4224]{1,0:T(8,128)(2,1)S(1)}, u32[]{:S(2)}, u32[]{:S(2)}) collective-permute-start(bf16[32,4224]{1,0:T(8,128)(2,1)} %get-tuple-element.105), channel_id=1, source_target_pairs={{0,192},{1,193},{2,194},{3,195},{4,196},{5,197},{6,198},{7,199},{8... | collective-permute-start | bytes 811016 | tf_op jit(solution)/shard_map/ppermute | solution.py:446
  332.4 11.8 %collective-permute-start.19 = (bf16[32,4224]{1,0:T(8,128)(2,1)}, bf16[32,4224]{1,0:T(8,128)(2,1)}, u32[]{:S(2)}, u32[]{:S(2)}) collective-permute-start(bf16[32,4224]{1,0:T(8,128)(2,1)} %get-tuple-element.106), channel_id=1, source_target_pairs={{0,200},{1,201},{2,202},{3,203},{4,204},{5,205},{6,206},{7,207},{8... | collective-permute-start | bytes 811016 | tf_op jit(solution)/shard_map/ppermute | solution.py:446
  332.5 15.4 %collective-permute-start.20 = (bf16[32,4224]{1,0:T(8,128)(2,1)}, bf16[32,4224]{1,0:T(8,128)(2,1)}, u32[]{:S(2)}, u32[]{:S(2)}) collective-permute-start(bf16[32,4224]{1,0:T(8,128)(2,1)} %get-tuple-element.107), channel_id=1, source_target_pairs={{0,208},{1,209},{2,210},{3,211},{4,212},{5,213},{6,214},{7,215},{8... | collective-permute-start | bytes 811016 | tf_op jit(solution)/shard_map/ppermute | solution.py:446
  336.0 22.7 %collective-permute-start.21 = (bf16[32,4224]{1,0:T(8,128)(2,1)}, bf16[32,4224]{1,0:T(8,128)(2,1)}, u32[]{:S(2)}, u32[]{:S(2)}) collective-permute-start(bf16[32,4224]{1,0:T(8,128)(2,1)} %get-tuple-element.108), channel_id=1, source_target_pairs={{0,216},{1,217},{2,218},{3,219},{4,220},{5,221},{6,222},{7,223},{8... | collective-permute-start | bytes 811016 | tf_op jit(solution)/shard_map/ppermute | solution.py:446
  363.0 8.1 %collective-permute-start.22 = (bf16[256,4224]{1,0:T(8,128)(2,1)}, bf16[256,4224]{1,0:T(8,128)(2,1)}, u32[]{:S(2)}, u32[]{:S(2)}) collective-permute-start(bf16[256,4224]{1,0:T(8,128)(2,1)} %stack.1), channel_id=1, source_target_pairs={{0,32},{1,33},{2,34},{3,35},{4,36},{5,37},{6,38},{7,39},{8,40},{9,... | collective-permute-start | bytes 6488072 | tf_op jit(solution)/shard_map/ppermute | solution.py:456
  (26 other events, 1121.3 us)
